TPU v7x, 32 devices: a 4x4x1 block of a 4x4x8 slice. The times are simulated.
32 devices in a mesh: data: 1 (over z), col: 4 (over y), row: 8 (over x, core).
Axes of the slice: x: 4, y: 4, z: 1, core: 2. Of those that a mesh axis runs over, the one named last changes fastest.
The devices are a block of a 4x4x8 slice.
Arguments:
- pair_rep: bfloat16 [768, 768, 128], P(('data', 'row'), 'col')
- res_mask: int32 [768], P('data')
- ln_gamma: float32 [128], replicated
- ln_beta: float32 [128], replicated
- w_q: bfloat16 [128, 128], replicated
- w_k: bfloat16 [128, 128], replicated
- w_v: bfloat16 [128, 128], replicated
- w_b: bfloat16 [128, 4], replicated
- w_g: bfloat16 [128, 128], replicated
- w_o: bfloat16 [128, 128], replicated
Outputs:
- output: bfloat16 [768, 768, 128], P(('data', 'row'), 'col')
All inputs are finite; a program needn't handle non-finite values.
Results may differ from a plain program's by a relative error of at most 0.00640002.
Values are sent between devices in bfloat16 or wider.
A program may use at most 768 MiB of HBM per device.

v0:
```python
import math
import jax
import jax.numpy as jnp
from jax import lax
from jax.sharding import PartitionSpec as P

LN_EPS = 1e-5
MASK_FILL = -1e9


def norm_and_project(pair_tile, ln_gamma, ln_beta, w_q, w_k, w_v, w_b, w_g):
    n_chan = pair_tile.shape[-1]
    heads = w_b.shape[1]
    head_dim = w_q.shape[1] // heads
    pair_f32 = pair_tile.astype(jnp.float32)
    mean = jnp.mean(pair_f32, axis=-1, keepdims=True)
    centred = pair_f32 - mean
    variance = jnp.mean(centred * centred, axis=-1, keepdims=True)
    normed = (centred * lax.rsqrt(variance + LN_EPS) * ln_gamma + ln_beta).astype(jnp.bfloat16)
    query = (jnp.einsum('ijc,chd->jhid', normed, w_q.reshape(n_chan, heads, head_dim), preferred_element_type=jnp.float32) * (1.0 / math.sqrt(head_dim))).astype(jnp.bfloat16)
    w_kv = jnp.stack([w_k.reshape(n_chan, heads, head_dim), w_v.reshape(n_chan, heads, head_dim)])
    kv_pair = jnp.einsum('ijc,echd->ejhid', normed, w_kv, preferred_element_type=jnp.float32).astype(jnp.bfloat16)
    gate = jax.nn.sigmoid(jnp.einsum('ijc,chd->jhid', normed, w_g.reshape(n_chan, heads, head_dim), preferred_element_type=jnp.float32))
    bias_tile = jnp.einsum('ijc,ch->ijh', normed, w_b, preferred_element_type=jnp.float32).astype(jnp.bfloat16)
    return pair_f32, query, kv_pair, gate, bias_tile


def bias_strip(bias_tile):
    full_cols = lax.all_gather(bias_tile, 'col', axis=1, tiled=True)
    own_rows = lax.all_to_all(full_cols, 'row', 1, 0, tiled=True)
    return jnp.transpose(own_rows, (2, 1, 0))


def attend_block(state, query, kv_blk, bias_blk, fill_blk):
    run_max, run_sum, out_acc = state
    logits = jnp.einsum('jhid,jhkd->jhik', query, kv_blk[0], preferred_element_type=jnp.float32) + bias_blk[None] + fill_blk
    new_max = jnp.maximum(run_max, jnp.max(logits, axis=-1))
    rescale = jnp.exp(run_max - new_max)
    p_exp = jnp.exp(logits - new_max[..., None])
    run_sum = run_sum * rescale + jnp.sum(p_exp, axis=-1)
    out_acc = out_acc * rescale[..., None] + jnp.einsum('jhik,jhkd->jhid', p_exp.astype(jnp.bfloat16), kv_blk[1], preferred_element_type=jnp.float32)
    return new_max, run_sum, out_acc


def finish(state, gate, pair_f32, w_o):
    run_max, run_sum, out_acc = state
    heads = gate.shape[1]
    head_dim = gate.shape[3]
    gated = (gate * (out_acc / run_sum[..., None])).astype(jnp.bfloat16)
    update = jnp.einsum('jhid,hdc->ijc', gated, w_o.reshape(heads, head_dim, w_o.shape[1]), preferred_element_type=jnp.float32)
    return (pair_f32 + update).astype(jnp.bfloat16)


def solution(mesh):
    rows = mesh.shape['row']
    next_hop = [(src_id, (src_id + 1) % rows) for src_id in range(rows)]

    def body(pair_tile, res_mask, ln_gamma, ln_beta, w_q, w_k, w_v, w_b, w_g, w_o):
        pair_f32, query, kv_pair, gate, bias_tile = norm_and_project(pair_tile, ln_gamma, ln_beta, w_q, w_k, w_v, w_b, w_g)
        strip = bias_strip(bias_tile)
        key_fill = jnp.where(res_mask > 0, 0.0, MASK_FILL).astype(jnp.float32)
        block = pair_tile.shape[0]
        my_row = lax.axis_index('row')

        def fold(step, state, kv_blk):
            key_lo = ((my_row - step) % rows) * block
            bias_blk = lax.dynamic_slice_in_dim(strip, key_lo, block, axis=2)
            fill_blk = lax.dynamic_slice_in_dim(key_fill, key_lo, block)
            return attend_block(state, query, kv_blk, bias_blk, fill_blk)

        stat_shape = query.shape[:3]
        state = (jnp.full(stat_shape, -jnp.inf, jnp.float32), jnp.zeros(stat_shape, jnp.float32), jnp.zeros(query.shape, jnp.float32))
        state = fold(0, state, kv_pair)

        def shift_step(step, carry):
            cur_state, kv_blk = carry
            kv_blk = lax.ppermute(kv_blk, 'row', next_hop)
            return fold(step, cur_state, kv_blk), kv_blk

        state, kv_last = lax.fori_loop(1, rows, shift_step, (state, kv_pair))
        return finish(state, gate, pair_f32, w_o)

    tile_spec = P(('data', 'row'), 'col', None)
    return jax.shard_map(body, mesh=mesh, in_specs=(tile_spec, P('data'), P(), P(), P(), P(), P(), P(), P(), P()), out_specs=tile_spec, check_vma=False)
```

profile of v0, /device:TPU:97, one launch (start us, length us, event | category | flops | bytes accessed | tf_op | source)
XLA Modules:
  0.0 1725.8 jit_solution(2009760479554788380)
XLA Ops:
  0.0 6.4 convert_reduce_fusion
  6.5 7.7 fusion.22
  14.3 11.4 convolution_convert_fusion
  25.8 15.1 all_gather.3
  40.8 6.8 all-to-all-start
  47.6 7.9 fusion.55
  55.8 10.3 convert_bitcast_fusion
  66.1 10.5 slice_bitcast_fusion.6
  76.6 24.9 %copy.74 = bf16[2,192,4,96,32]{3,4,2,1,0:T(8,128)(2,1)} copy(bf16[2,192,4,96,32]{1,4,3,2,0:T(8,128)(2,1)} %convert_bitcast_fusion) | data formatting | bytes 18874368 | tf_op jit(solution)/shard_map/while | solution.py:80
  101.4 13.4 copy.70
  115.0 8.4 fusion.27
  123.4 13.5 copy.69
  136.9 13.6 copy.73
  150.5 0.7 copy.63
  151.3 0.6 copy.71
  152.0 18.7 %fusion.11 = (f32[192,4,96]{2,1,0:T(4,128)S(1)}, f32[192,4,96,96]{2,3,1,0:T(8,128)}) fusion(f32[96]{0:T(128)S(1)} %dynamic_slice.27, f32[4,96,96]{1,2,0:T(8,128)S(1)} %convert_bitcast_fusion.1, bf16[192,4,96,32]{2,3,1,0:T(8,128)(2,1)} %copy.69, bf16[192,4,96,32]{2,3,1,0:T(8,128)(2,1)} %copy.70), kind=kOutput, calls=%fused_computation.18 | convolution fusion | flops 474144768 | bytes 38191488 | tf_op jit(solution)/shard_map/jhid,jhkd->jhik/dot_general | solution.py:36
  170.6 18.9 %fusion.13 = f32[192,4,96]{2,1,0:T(4,128)S(1)} fusion(f32[192,4,96,96]{2,3,1,0:T(8,128)} %get-tuple-element.294, f32[192,4,96]{2,1,0:T(4,128)S(1)} %get-tuple-element.363, f32[96]{0:T(128)S(1)} %dynamic_slice.27, f32[4,96,96]{1,2,0:T(8,128)S(1)} %convert_bitcast_fusion.1), kind=kLoop, calls=%fused_computation.20 | loop fusion | flops 28237824 | bytes 29049216 | tf_op jit(solution)/shard_map/reduce_sum | solution.py:40
  189.7 21.4 %broadcast_add_fusion = f32[192,4,96,32]{2,3,1,0:T(8,128)} fusion(f32[192,4,96]{2,1,0:T(4,128)S(1)} %get-tuple-element.291, bf16[192,4,96,32]{2,3,1,0:T(8,128)(2,1)} %copy.73, f32[192,4,96,96]{2,3,1,0:T(8,128)} %get-tuple-element.294, f32[192,4,96]{2,1,0:T(4,128)S(1)} %get-tuple-element.363, f32[96]{0:T(128)S(1)} %dynamic_slice.27, ...), kind=kOutput, calls=%fused_computation.42 | convolution fusion | flops 483655680 | bytes 43204992 | tf_op jit(solution)/shard_map/jhik,jhkd->jhid/dot_general | solution.py:41
  211.2 1488.1 %while.21 = (s32[]{:T(128)}, f32[192,4,96]{2,1,0:T(4,128)S(1)}, f32[192,4,96]{2,1,0:T(4,128)S(1)}, f32[192,4,96,32]{2,3,1,0:T(8,128)}, bf16[2,192,4,96,32]{3,4,2...) while((s32[]{:T(128)}, f32[192,4,96]{2,1,0:T(4,128)S(1)}, ...), condition=%wide.region_7.8_spmd, body=%wide.region_4.7_spmd.sunk | while | flops 988729344 | bytes 197273840 | solution.py:80
  211.6 1.7 collective-permute-start
  213.4 135.2 %collective-permute-done = bf16[2,192,4,96,32]{3,4,2,1,0:T(8,128)(2,1)} collective-permute-done((bf16[2,192,4,96,32]{3,4,2,1,0:T(8,128)(2,1)}, bf16[2,192,4,96,32]{3,4,2,1,0:T(8,128)(2,1)}, u32[]{:S(2)}, u32[]{:S(2)}) %collective-permute-start) | collective-permute-done | bytes 9437216 | tf_op jit(solution)/shard_map/while/body/eval_jaxpr/ppermute | solution.py:77
  348.6 18.7 %fusion.71 = (f32[192,4,96]{2,1,0:T(4,128)S(1)}, f32[192,4,96,96]{2,3,1,0:T(8,128)}) fusion(f32[96]{0:T(128)S(1)} %dynamic_slice.33, f32[4,96,96]{1,2,0:T(8,128)S(1)} %dynamic-slice_convert_fusion.2, bf16[192,4,96,32]{2,3,1,0:T(8,128)(2,1)} %get-tuple-element.397, bf16[2,192,4,96,32]{3,4,2,1,0:T(8,128)(2,1)} %collective-permute-done), kind=kOutput, calls=%fused_computation.2.clone.1 | convolution fusion | flops 474144768 | bytes 41337216 | tf_op jit(solution)/shard_map/while/body/eval_jaxpr/jhid,jhkd->jhik/dot_general | solution.py:36
  367.4 18.9 %fusion.72 = f32[192,4,96]{2,1,0:T(4,128)S(1)} fusion(f32[192,4,96,96]{2,3,1,0:T(8,128)} %get-tuple-element.359, f32[192,4,96]{2,1,0:T(4,128)S(1)} %max.11, f32[96]{0:T(128)S(1)} %dynamic_slice.33, f32[4,96,96]{1,2,0:T(8,128)S(1)} %dynamic-slice_convert_fusion.2), kind=kLoop, calls=%fused_computation.4.clone.1 | loop fusion | flops 28237824 | bytes 29049216 | tf_op jit(solution)/shard_map/while/body/eval_jaxpr/reduce_sum | solution.py:40
  386.3 0.3 multiply_add_fusion.4
  386.6 11.8 copy.121
  398.4 25.0 %multiply_add_fusion.5 = f32[192,4,96,32]{2,3,1,0:T(8,128)} fusion(f32[192,4,96,32]{2,3,1,0:T(8,128)} %get-tuple-element.380, f32[192,4,96]{2,1,0:T(4,128)S(1)} %bitcast.106, f32[192,4,96,96]{2,3,1,0:T(8,128)} %get-tuple-element.359, f32[192,4,96]{2,1,0:T(4,128)S(1)} %max.11, f32[96]{0:T(128)S(1)} %dynamic_slice.33, ...), kind=kOutput, calls=%fused_computation.9.clone.1 | convolution fusion | flops 486014976 | bytes 66797952 | tf_op jit(solution)/shard_map/while/body/eval_jaxpr/jhik,jhkd->jhid/dot_general | solution.py:41
  423.4 2.5 collective-permute-start
  426.0 135.2 %collective-permute-done = bf16[2,192,4,96,32]{3,4,2,1,0:T(8,128)(2,1)} collective-permute-done((bf16[2,192,4,96,32]{3,4,2,1,0:T(8,128)(2,1)}, bf16[2,192,4,96,32]{3,4,2,1,0:T(8,128)(2,1)}, u32[]{:S(2)}, u32[]{:S(2)}) %collective-permute-start) | collective-permute-done | bytes 9437216 | tf_op jit(solution)/shard_map/while/body/eval_jaxpr/ppermute | solution.py:77
  561.2 18.7 %fusion.71 = (f32[192,4,96]{2,1,0:T(4,128)S(1)}, f32[192,4,96,96]{2,3,1,0:T(8,128)}) fusion(f32[96]{0:T(128)S(1)} %dynamic_slice.33, f32[4,96,96]{1,2,0:T(8,128)S(1)} %dynamic-slice_convert_fusion.2, bf16[192,4,96,32]{2,3,1,0:T(8,128)(2,1)} %get-tuple-element.397, bf16[2,192,4,96,32]{3,4,2,1,0:T(8,128)(2,1)} %collective-permute-done), kind=kOutput, calls=%fused_computation.2.clone.1 | convolution fusion | flops 474144768 | bytes 41337216 | tf_op jit(solution)/shard_map/while/body/eval_jaxpr/jhid,jhkd->jhik/dot_general | solution.py:36
  580.0 18.9 %fusion.72 = f32[192,4,96]{2,1,0:T(4,128)S(1)} fusion(f32[192,4,96,96]{2,3,1,0:T(8,128)} %get-tuple-element.359, f32[192,4,96]{2,1,0:T(4,128)S(1)} %max.11, f32[96]{0:T(128)S(1)} %dynamic_slice.33, f32[4,96,96]{1,2,0:T(8,128)S(1)} %dynamic-slice_convert_fusion.2), kind=kLoop, calls=%fused_computation.4.clone.1 | loop fusion | flops 28237824 | bytes 29049216 | tf_op jit(solution)/shard_map/while/body/eval_jaxpr/reduce_sum | solution.py:40
  599.3 11.8 copy.121
  611.0 25.0 %multiply_add_fusion.5 = f32[192,4,96,32]{2,3,1,0:T(8,128)} fusion(f32[192,4,96,32]{2,3,1,0:T(8,128)} %get-tuple-element.380, f32[192,4,96]{2,1,0:T(4,128)S(1)} %bitcast.106, f32[192,4,96,96]{2,3,1,0:T(8,128)} %get-tuple-element.359, f32[192,4,96]{2,1,0:T(4,128)S(1)} %max.11, f32[96]{0:T(128)S(1)} %dynamic_slice.33, ...), kind=kOutput, calls=%fused_computation.9.clone.1 | convolution fusion | flops 486014976 | bytes 66797952 | tf_op jit(solution)/shard_map/while/body/eval_jaxpr/jhik,jhkd->jhid/dot_general | solution.py:41
  636.1 2.5 collective-permute-start
  638.7 135.2 %collective-permute-done = bf16[2,192,4,96,32]{3,4,2,1,0:T(8,128)(2,1)} collective-permute-done((bf16[2,192,4,96,32]{3,4,2,1,0:T(8,128)(2,1)}, bf16[2,192,4,96,32]{3,4,2,1,0:T(8,128)(2,1)}, u32[]{:S(2)}, u32[]{:S(2)}) %collective-permute-start) | collective-permute-done | bytes 9437216 | tf_op jit(solution)/shard_map/while/body/eval_jaxpr/ppermute | solution.py:77
  773.9 18.7 %fusion.71 = (f32[192,4,96]{2,1,0:T(4,128)S(1)}, f32[192,4,96,96]{2,3,1,0:T(8,128)}) fusion(f32[96]{0:T(128)S(1)} %dynamic_slice.33, f32[4,96,96]{1,2,0:T(8,128)S(1)} %dynamic-slice_convert_fusion.2, bf16[192,4,96,32]{2,3,1,0:T(8,128)(2,1)} %get-tuple-element.397, bf16[2,192,4,96,32]{3,4,2,1,0:T(8,128)(2,1)} %collective-permute-done), kind=kOutput, calls=%fused_computation.2.clone.1 | convolution fusion | flops 474144768 | bytes 41337216 | tf_op jit(solution)/shard_map/while/body/eval_jaxpr/jhid,jhkd->jhik/dot_general | solution.py:36
  792.7 18.9 %fusion.72 = f32[192,4,96]{2,1,0:T(4,128)S(1)} fusion(f32[192,4,96,96]{2,3,1,0:T(8,128)} %get-tuple-element.359, f32[192,4,96]{2,1,0:T(4,128)S(1)} %max.11, f32[96]{0:T(128)S(1)} %dynamic_slice.33, f32[4,96,96]{1,2,0:T(8,128)S(1)} %dynamic-slice_convert_fusion.2), kind=kLoop, calls=%fused_computation.4.clone.1 | loop fusion | flops 28237824 | bytes 29049216 | tf_op jit(solution)/shard_map/while/body/eval_jaxpr/reduce_sum | solution.py:40
  811.9 11.8 copy.121
  823.7 25.0 %multiply_add_fusion.5 = f32[192,4,96,32]{2,3,1,0:T(8,128)} fusion(f32[192,4,96,32]{2,3,1,0:T(8,128)} %get-tuple-element.380, f32[192,4,96]{2,1,0:T(4,128)S(1)} %bitcast.106, f32[192,4,96,96]{2,3,1,0:T(8,128)} %get-tuple-element.359, f32[192,4,96]{2,1,0:T(4,128)S(1)} %max.11, f32[96]{0:T(128)S(1)} %dynamic_slice.33, ...), kind=kOutput, calls=%fused_computation.9.clone.1 | convolution fusion | flops 486014976 | bytes 66797952 | tf_op jit(solution)/shard_map/while/body/eval_jaxpr/jhik,jhkd->jhid/dot_general | solution.py:41
  848.7 2.5 collective-permute-start
  851.3 135.2 %collective-permute-done = bf16[2,192,4,96,32]{3,4,2,1,0:T(8,128)(2,1)} collective-permute-done((bf16[2,192,4,96,32]{3,4,2,1,0:T(8,128)(2,1)}, bf16[2,192,4,96,32]{3,4,2,1,0:T(8,128)(2,1)}, u32[]{:S(2)}, u32[]{:S(2)}) %collective-permute-start) | collective-permute-done | bytes 9437216 | tf_op jit(solution)/shard_map/while/body/eval_jaxpr/ppermute | solution.py:77
  986.5 18.7 %fusion.71 = (f32[192,4,96]{2,1,0:T(4,128)S(1)}, f32[192,4,96,96]{2,3,1,0:T(8,128)}) fusion(f32[96]{0:T(128)S(1)} %dynamic_slice.33, f32[4,96,96]{1,2,0:T(8,128)S(1)} %dynamic-slice_convert_fusion.2, bf16[192,4,96,32]{2,3,1,0:T(8,128)(2,1)} %get-tuple-element.397, bf16[2,192,4,96,32]{3,4,2,1,0:T(8,128)(2,1)} %collective-permute-done), kind=kOutput, calls=%fused_computation.2.clone.1 | convolution fusion | flops 474144768 | bytes 41337216 | tf_op jit(solution)/shard_map/while/body/eval_jaxpr/jhid,jhkd->jhik/dot_general | solution.py:36
  1005.3 18.9 %fusion.72 = f32[192,4,96]{2,1,0:T(4,128)S(1)} fusion(f32[192,4,96,96]{2,3,1,0:T(8,128)} %get-tuple-element.359, f32[192,4,96]{2,1,0:T(4,128)S(1)} %max.11, f32[96]{0:T(128)S(1)} %dynamic_slice.33, f32[4,96,96]{1,2,0:T(8,128)S(1)} %dynamic-slice_convert_fusion.2), kind=kLoop, calls=%fused_computation.4.clone.1 | loop fusion | flops 28237824 | bytes 29049216 | tf_op jit(solution)/shard_map/while/body/eval_jaxpr/reduce_sum | solution.py:40
  1024.5 11.8 copy.121
  1036.3 25.0 %multiply_add_fusion.5 = f32[192,4,96,32]{2,3,1,0:T(8,128)} fusion(f32[192,4,96,32]{2,3,1,0:T(8,128)} %get-tuple-element.380, f32[192,4,96]{2,1,0:T(4,128)S(1)} %bitcast.106, f32[192,4,96,96]{2,3,1,0:T(8,128)} %get-tuple-element.359, f32[192,4,96]{2,1,0:T(4,128)S(1)} %max.11, f32[96]{0:T(128)S(1)} %dynamic_slice.33, ...), kind=kOutput, calls=%fused_computation.9.clone.1 | convolution fusion | flops 486014976 | bytes 66797952 | tf_op jit(solution)/shard_map/while/body/eval_jaxpr/jhik,jhkd->jhid/dot_general | solution.py:41
  1061.4 2.5 collective-permute-start
  1064.0 135.2 %collective-permute-done = bf16[2,192,4,96,32]{3,4,2,1,0:T(8,128)(2,1)} collective-permute-done((bf16[2,192,4,96,32]{3,4,2,1,0:T(8,128)(2,1)}, bf16[2,192,4,96,32]{3,4,2,1,0:T(8,128)(2,1)}, u32[]{:S(2)}, u32[]{:S(2)}) %collective-permute-start) | collective-permute-done | bytes 9437216 | tf_op jit(solution)/shard_map/while/body/eval_jaxpr/ppermute | solution.py:77
  1199.2 18.7 %fusion.71 = (f32[192,4,96]{2,1,0:T(4,128)S(1)}, f32[192,4,96,96]{2,3,1,0:T(8,128)}) fusion(f32[96]{0:T(128)S(1)} %dynamic_slice.33, f32[4,96,96]{1,2,0:T(8,128)S(1)} %dynamic-slice_convert_fusion.2, bf16[192,4,96,32]{2,3,1,0:T(8,128)(2,1)} %get-tuple-element.397, bf16[2,192,4,96,32]{3,4,2,1,0:T(8,128)(2,1)} %collective-permute-done), kind=kOutput, calls=%fused_computation.2.clone.1 | convolution fusion | flops 474144768 | bytes 41337216 | tf_op jit(solution)/shard_map/while/body/eval_jaxpr/jhid,jhkd->jhik/dot_general | solution.py:36
  1218.0 18.9 %fusion.72 = f32[192,4,96]{2,1,0:T(4,128)S(1)} fusion(f32[192,4,96,96]{2,3,1,0:T(8,128)} %get-tuple-element.359, f32[192,4,96]{2,1,0:T(4,128)S(1)} %max.11, f32[96]{0:T(128)S(1)} %dynamic_slice.33, f32[4,96,96]{1,2,0:T(8,128)S(1)} %dynamic-slice_convert_fusion.2), kind=kLoop, calls=%fused_computation.4.clone.1 | loop fusion | flops 28237824 | bytes 29049216 | tf_op jit(solution)/shard_map/while/body/eval_jaxpr/reduce_sum | solution.py:40
  1237.2 11.8 copy.121
  1249.0 25.0 %multiply_add_fusion.5 = f32[192,4,96,32]{2,3,1,0:T(8,128)} fusion(f32[192,4,96,32]{2,3,1,0:T(8,128)} %get-tuple-element.380, f32[192,4,96]{2,1,0:T(4,128)S(1)} %bitcast.106, f32[192,4,96,96]{2,3,1,0:T(8,128)} %get-tuple-element.359, f32[192,4,96]{2,1,0:T(4,128)S(1)} %max.11, f32[96]{0:T(128)S(1)} %dynamic_slice.33, ...), kind=kOutput, calls=%fused_computation.9.clone.1 | convolution fusion | flops 486014976 | bytes 66797952 | tf_op jit(solution)/shard_map/while/body/eval_jaxpr/jhik,jhkd->jhid/dot_general | solution.py:41
  1274.0 2.5 collective-permute-start
  1276.6 135.2 %collective-permute-done = bf16[2,192,4,96,32]{3,4,2,1,0:T(8,128)(2,1)} collective-permute-done((bf16[2,192,4,96,32]{3,4,2,1,0:T(8,128)(2,1)}, bf16[2,192,4,96,32]{3,4,2,1,0:T(8,128)(2,1)}, u32[]{:S(2)}, u32[]{:S(2)}) %collective-permute-start) | collective-permute-done | bytes 9437216 | tf_op jit(solution)/shard_map/while/body/eval_jaxpr/ppermute | solution.py:77
  1411.8 18.7 %fusion.71 = (f32[192,4,96]{2,1,0:T(4,128)S(1)}, f32[192,4,96,96]{2,3,1,0:T(8,128)}) fusion(f32[96]{0:T(128)S(1)} %dynamic_slice.33, f32[4,96,96]{1,2,0:T(8,128)S(1)} %dynamic-slice_convert_fusion.2, bf16[192,4,96,32]{2,3,1,0:T(8,128)(2,1)} %get-tuple-element.397, bf16[2,192,4,96,32]{3,4,2,1,0:T(8,128)(2,1)} %collective-permute-done), kind=kOutput, calls=%fused_computation.2.clone.1 | convolution fusion | flops 474144768 | bytes 41337216 | tf_op jit(solution)/shard_map/while/body/eval_jaxpr/jhid,jhkd->jhik/dot_general | solution.py:36
  1430.6 18.9 %fusion.72 = f32[192,4,96]{2,1,0:T(4,128)S(1)} fusion(f32[192,4,96,96]{2,3,1,0:T(8,128)} %get-tuple-element.359, f32[192,4,96]{2,1,0:T(4,128)S(1)} %max.11, f32[96]{0:T(128)S(1)} %dynamic_slice.33, f32[4,96,96]{1,2,0:T(8,128)S(1)} %dynamic-slice_convert_fusion.2), kind=kLoop, calls=%fused_computation.4.clone.1 | loop fusion | flops 28237824 | bytes 29049216 | tf_op jit(solution)/shard_map/while/body/eval_jaxpr/reduce_sum | solution.py:40
  1449.8 11.8 copy.121
  1461.6 25.0 %multiply_add_fusion.5 = f32[192,4,96,32]{2,3,1,0:T(8,128)} fusion(f32[192,4,96,32]{2,3,1,0:T(8,128)} %get-tuple-element.380, f32[192,4,96]{2,1,0:T(4,128)S(1)} %bitcast.106, f32[192,4,96,96]{2,3,1,0:T(8,128)} %get-tuple-element.359, f32[192,4,96]{2,1,0:T(4,128)S(1)} %max.11, f32[96]{0:T(128)S(1)} %dynamic_slice.33, ...), kind=kOutput, calls=%fused_computation.9.clone.1 | convolution fusion | flops 486014976 | bytes 66797952 | tf_op jit(solution)/shard_map/while/body/eval_jaxpr/jhik,jhkd->jhid/dot_general | solution.py:41
  1486.7 2.5 collective-permute-start
  1489.3 135.2 %collective-permute-done = bf16[2,192,4,96,32]{3,4,2,1,0:T(8,128)(2,1)} collective-permute-done((bf16[2,192,4,96,32]{3,4,2,1,0:T(8,128)(2,1)}, bf16[2,192,4,96,32]{3,4,2,1,0:T(8,128)(2,1)}, u32[]{:S(2)}, u32[]{:S(2)}) %collective-permute-start) | collective-permute-done | bytes 9437216 | tf_op jit(solution)/shard_map/while/body/eval_jaxpr/ppermute | solution.py:77
  1624.5 18.7 %fusion.71 = (f32[192,4,96]{2,1,0:T(4,128)S(1)}, f32[192,4,96,96]{2,3,1,0:T(8,128)}) fusion(f32[96]{0:T(128)S(1)} %dynamic_slice.33, f32[4,96,96]{1,2,0:T(8,128)S(1)} %dynamic-slice_convert_fusion.2, bf16[192,4,96,32]{2,3,1,0:T(8,128)(2,1)} %get-tuple-element.397, bf16[2,192,4,96,32]{3,4,2,1,0:T(8,128)(2,1)} %collective-permute-done), kind=kOutput, calls=%fused_computation.2.clone.1 | convolution fusion | flops 474144768 | bytes 41337216 | tf_op jit(solution)/shard_map/while/body/eval_jaxpr/jhid,jhkd->jhik/dot_general | solution.py:36
  1643.2 18.9 %fusion.72 = f32[192,4,96]{2,1,0:T(4,128)S(1)} fusion(f32[192,4,96,96]{2,3,1,0:T(8,128)} %get-tuple-element.359, f32[192,4,96]{2,1,0:T(4,128)S(1)} %max.11, f32[96]{0:T(128)S(1)} %dynamic_slice.33, f32[4,96,96]{1,2,0:T(8,128)S(1)} %dynamic-slice_convert_fusion.2), kind=kLoop, calls=%fused_computation.4.clone.1 | loop fusion | flops 28237824 | bytes 29049216 | tf_op jit(solution)/shard_map/while/body/eval_jaxpr/reduce_sum | solution.py:40
  1662.5 11.8 copy.121
  1674.3 25.0 %multiply_add_fusion.5 = f32[192,4,96,32]{2,3,1,0:T(8,128)} fusion(f32[192,4,96,32]{2,3,1,0:T(8,128)} %get-tuple-element.380, f32[192,4,96]{2,1,0:T(4,128)S(1)} %bitcast.106, f32[192,4,96,96]{2,3,1,0:T(8,128)} %get-tuple-element.359, f32[192,4,96]{2,1,0:T(4,128)S(1)} %max.11, f32[96]{0:T(128)S(1)} %dynamic_slice.33, ...), kind=kOutput, calls=%fused_computation.9.clone.1 | convolution fusion | flops 486014976 | bytes 66797952 | tf_op jit(solution)/shard_map/while/body/eval_jaxpr/jhik,jhkd->jhid/dot_general | solution.py:41
  1699.4 19.9 %fusion.26 = bf16[96,192,128]{2,0,1:T(8,128)(2,1)} fusion(bf16[96,192,128]{2,1,0:T(8,128)(2,1)} %param.12, bf16[4,32,128,1]{2,1,0,3:T(8,128)(2,1)S(1)} %bitcast.103, f32[192,4,96,32]{2,3,1,0:T(8,128)} %get-tuple-element.227, f32[192,4,96]{2,1,0:T(4,128)S(1)} %get-tuple-element.228, bf16[128,4,32,1]{0,2,1,3:T(8,128)(2,1)S(1)} %bitcast.116, ...), kind=kOutput, calls=%fused_computation.38 | convolution fusion | flops 1243348992 | bytes 19383296 | tf_op jit(solution)/shard_map/jhid,hdc->ijc/dot_general | solution.py:50
  1719.3 6.3 copy.76
  (78 shorter events, 4.1 us)
Async XLA Ops:
  0.0 1699.3 %copy-start = (bf16[128,128]{1,0:T(8,128)(2,1)S(1)}, bf16[128,128]{1,0:T(8,128)(2,1)}, u32[]{:S(2)}) copy-start(bf16[128,128]{1,0:T(8,128)(2,1)} %param.21) | copy-start | bytes 98308
  0.0 14.3 copy-start.1
  0.0 14.3 copy-start.14
  0.0 14.3 copy-start.12
  0.0 14.3 copy-start.16
  6.5 41.1 %copy-start.2 = (f32[96,192]{0,1:T(8,128)}, f32[96,192]{0,1:T(8,128)S(1)}, u32[]{:S(2)}) copy-start(f32[96,192]{0,1:T(8,128)S(1)} %broadcast_multiply_fusion) | copy-start | bytes 221188
  14.3 41.2 %copy-start.4 = (f32[96,192]{0,1:T(8,128)}, f32[96,192]{0,1:T(8,128)S(1)}, u32[]{:S(2)}) copy-start(f32[96,192]{0,1:T(8,128)S(1)} %add_rsqrt_fusion) | copy-start | bytes 221188
  25.7 29.8 %copy-start.6 = (bf16[128,128]{1,0:T(8,128)(2,1)S(1)}, bf16[128,128]{1,0:T(8,128)(2,1)}, u32[]{:S(2)}) copy-start(bf16[128,128]{1,0:T(8,128)(2,1)} %param.17) | copy-start | bytes 98308
  25.7 29.9 %copy-start.7 = (bf16[128,128]{1,0:T(8,128)(2,1)S(1)}, bf16[128,128]{1,0:T(8,128)(2,1)}, u32[]{:S(2)}) copy-start(bf16[128,128]{1,0:T(8,128)(2,1)} %param.18) | copy-start | bytes 98308
  40.8 110.4 %all-to-all-start = ((bf16[96,768,4]{0,2,1:T(4,128)(2,1)}), bf16[96,768,4]{0,2,1:T(4,128)(2,1)S(1)}, u32[]{:S(2)}, u32[]{:S(2)}) async-start(bf16[96,768,4]{0,2,1:T(4,128)(2,1)} %all_gather.3), calls=%async_computation | async-start | bytes 1572864 | tf_op jit(solution)/shard_map/all_to_all | solution.py:30
  101.4 13.4 copy-start.8
  136.8 13.6 copy-start.9
  136.9 14.3 copy-start.11
  211.2 1488.1 %copy-start.3 = (f32[96,192]{0,1:T(8,128)S(1)}, f32[96,192]{0,1:T(8,128)}, u32[]{:S(2)}) copy-start(f32[96,192]{0,1:T(8,128)} %copy-done.2) | copy-start | bytes 221188
  211.2 1488.1 %copy-start.5 = (f32[96,192]{0,1:T(8,128)S(1)}, f32[96,192]{0,1:T(8,128)}, u32[]{:S(2)}) copy-start(f32[96,192]{0,1:T(8,128)} %copy-done.4) | copy-start | bytes 221188
  211.2 1488.2 %copy-start.10 = (bf16[128,128]{0,1:T(8,128)(2,1)S(1)}, bf16[128,128]{0,1:T(8,128)(2,1)}, u32[]{:S(2)}) copy-start(bf16[128,128]{0,1:T(8,128)(2,1)} %copy.63) | copy-start | bytes 98308
  211.2 1488.2 %copy-start.13 = (f32[128]{0:T(128)S(1)}, f32[128]{0:T(128)}, u32[]{:S(2)}) copy-start(f32[128]{0:T(128)} %param.15) | copy-start | bytes 1540
  211.2 1488.2 %copy-start.15 = (f32[128]{0:T(128)S(1)}, f32[128]{0:T(128)}, u32[]{:S(2)}) copy-start(f32[128]{0:T(128)} %param.14) | copy-start | bytes 1540
  211.6 137.0 %collective-permute-start = (bf16[2,192,4,96,32]{3,4,2,1,0:T(8,128)(2,1)}, bf16[2,192,4,96,32]{3,4,2,1,0:T(8,128)(2,1)}, u32[]{:S(2)}, u32[]{:S(2)}) collective-permute-start(bf16[2,192,4,96,32]{3,4,2,1,0:T(8,128)(2,1)} %get-tuple-element.381), channel_id=1, source_target_pairs={{0,1},{1,2},{2,3},{3,4},{4,5},{5,6},{6,7},{7,0},{8,9},{9,10},{10,1... | collective-permute-start | bytes 28311560 | tf_op jit(solution)/shard_map/while/body/eval_jaxpr/ppermute | solution.py:77
  423.4 137.8 %collective-permute-start = (bf16[2,192,4,96,32]{3,4,2,1,0:T(8,128)(2,1)}, bf16[2,192,4,96,32]{3,4,2,1,0:T(8,128)(2,1)}, u32[]{:S(2)}, u32[]{:S(2)}) collective-permute-start(bf16[2,192,4,96,32]{3,4,2,1,0:T(8,128)(2,1)} %get-tuple-element.381), channel_id=1, source_target_pairs={{0,1},{1,2},{2,3},{3,4},{4,5},{5,6},{6,7},{7,0},{8,9},{9,10},{10,1... | collective-permute-start | bytes 28311560 | tf_op jit(solution)/shard_map/while/body/eval_jaxpr/ppermute | solution.py:77
  636.1 137.8 %collective-permute-start = (bf16[2,192,4,96,32]{3,4,2,1,0:T(8,128)(2,1)}, bf16[2,192,4,96,32]{3,4,2,1,0:T(8,128)(2,1)}, u32[]{:S(2)}, u32[]{:S(2)}) collective-permute-start(bf16[2,192,4,96,32]{3,4,2,1,0:T(8,128)(2,1)} %get-tuple-element.381), channel_id=1, source_target_pairs={{0,1},{1,2},{2,3},{3,4},{4,5},{5,6},{6,7},{7,0},{8,9},{9,10},{10,1... | collective-permute-start | bytes 28311560 | tf_op jit(solution)/shard_map/while/body/eval_jaxpr/ppermute | solution.py:77
  848.7 137.8 %collective-permute-start = (bf16[2,192,4,96,32]{3,4,2,1,0:T(8,128)(2,1)}, bf16[2,192,4,96,32]{3,4,2,1,0:T(8,128)(2,1)}, u32[]{:S(2)}, u32[]{:S(2)}) collective-permute-start(bf16[2,192,4,96,32]{3,4,2,1,0:T(8,128)(2,1)} %get-tuple-element.381), channel_id=1, source_target_pairs={{0,1},{1,2},{2,3},{3,4},{4,5},{5,6},{6,7},{7,0},{8,9},{9,10},{10,1... | collective-permute-start | bytes 28311560 | tf_op jit(solution)/shard_map/while/body/eval_jaxpr/ppermute | solution.py:77
  1061.4 137.8 %collective-permute-start = (bf16[2,192,4,96,32]{3,4,2,1,0:T(8,128)(2,1)}, bf16[2,192,4,96,32]{3,4,2,1,0:T(8,128)(2,1)}, u32[]{:S(2)}, u32[]{:S(2)}) collective-permute-start(bf16[2,192,4,96,32]{3,4,2,1,0:T(8,128)(2,1)} %get-tuple-element.381), channel_id=1, source_target_pairs={{0,1},{1,2},{2,3},{3,4},{4,5},{5,6},{6,7},{7,0},{8,9},{9,10},{10,1... | collective-permute-start | bytes 28311560 | tf_op jit(solution)/shard_map/while/body/eval_jaxpr/ppermute | solution.py:77
  1274.0 137.8 %collective-permute-start = (bf16[2,192,4,96,32]{3,4,2,1,0:T(8,128)(2,1)}, bf16[2,192,4,96,32]{3,4,2,1,0:T(8,128)(2,1)}, u32[]{:S(2)}, u32[]{:S(2)}) collective-permute-start(bf16[2,192,4,96,32]{3,4,2,1,0:T(8,128)(2,1)} %get-tuple-element.381), channel_id=1, source_target_pairs={{0,1},{1,2},{2,3},{3,4},{4,5},{5,6},{6,7},{7,0},{8,9},{9,10},{10,1... | collective-permute-start | bytes 28311560 | tf_op jit(solution)/shard_map/while/body/eval_jaxpr/ppermute | solution.py:77
  1486.7 137.8 %collective-permute-start = (bf16[2,192,4,96,32]{3,4,2,1,0:T(8,128)(2,1)}, bf16[2,192,4,96,32]{3,4,2,1,0:T(8,128)(2,1)}, u32[]{:S(2)}, u32[]{:S(2)}) collective-permute-start(bf16[2,192,4,96,32]{3,4,2,1,0:T(8,128)(2,1)} %get-tuple-element.381), channel_id=1, source_target_pairs={{0,1},{1,2},{2,3},{3,4},{4,5},{5,6},{6,7},{7,0},{8,9},{9,10},{10,1... | collective-permute-start | bytes 28311560 | tf_op jit(solution)/shard_map/while/body/eval_jaxpr/ppermute | solution.py:77
where the time goes:
time: 1740 us; the launch traced here: 1730 us
  waiting for transfers between devices  947 us (54%)
  matrix products  396 us (23%)
  other arithmetic  176 us (10%)
  local copies, waits for them, and re-layouts  167 us (10%)
  starting transfers between devices  23.4 us (1%)
    ppermute x7, waiting for transfers between devices, shift_step(): kv_blk = lax.ppermute(kv_blk, 'row', next_hop)  947 us
    dot_general x8, matrix products, attend_block(): jnp.einsum('jhik,jhkd->jhid', p_exp.astype(jnp.bfloat16), kv_blk[1], pref...  197 us
    reduce_sum x8, other arithmetic, attend_block(): run_sum = run_sum * rescale + jnp.sum(p_exp, axis=-1)  151 us
    dot_general x8, matrix products, attend_block(): jnp.einsum('jhid,jhkd->jhik', query, kv_blk[0], preferred_element_type=jn...  149 us
    while x14, local copies, waits for them, and re-layouts  82.7 us
  transfers between devices with their start and end apart: 8, of which 7 were waited for; matrix products, arithmetic and copies ran while one was open for 6% of the time, Pallas kernels for 0%

commit v1 on v0

v1 whole, which is shorter than its diff:
```python
import functools
import math
import jax
import jax.numpy as jnp
from jax import lax
from jax.experimental import pallas as pl
from jax.experimental.pallas import tpu as pltpu
from jax.sharding import PartitionSpec as P

LN_EPS = 1e-5
MASK_FILL = -1e9
GROUP = 8
BLOCK = 256
F32 = jnp.float32
BF16 = jnp.bfloat16
NT = (((1,), (1,)), ((), ()))
TN = (((0,), (0,)), ((), ()))


def layer_norm(z, gamma, beta):
    mean = jnp.mean(z, axis=-1, keepdims=True)
    centred = z - mean
    variance = jnp.mean(centred * centred, axis=-1, keepdims=True)
    return centred * lax.rsqrt(variance + LN_EPS) * gamma + beta


def norm_group(z_ref, gamma, beta, a_scr, step=64):
    rows = z_ref.shape[0]

    def one(t, _):
        lo = pl.multiple_of(t * step, step)
        a = layer_norm(z_ref[pl.ds(lo, step)].astype(F32), gamma, beta)
        a_scr[pl.ds(pl.multiple_of(lo * GROUP, step * GROUP), step * GROUP), :] = a.reshape(step * GROUP, a.shape[-1])
        return 0

    lax.fori_loop(0, rows // step, one, 0)


def project_group(rows, a_scr, w_k, w_qvg_t, k_scr, q_scr, v_scr, g_scr, head_dim):
    proj = w_k.shape[1]

    def one(j, _):
        a = a_scr[pl.ds(j, rows, stride=GROUP), :].astype(BF16)
        k_scr[j] = jnp.dot(a, w_k[...], preferred_element_type=F32).astype(BF16)
        for lo in range(0, rows, BLOCK):
            t = lax.dot_general(w_qvg_t[...], a[lo:lo + BLOCK], NT, preferred_element_type=F32)
            q_scr[j, :, lo:lo + BLOCK] = (t[:proj] * (1.0 / math.sqrt(head_dim))).astype(BF16)
            v_scr[j, :, lo:lo + BLOCK] = t[proj:2 * proj].astype(BF16)
            g_scr[j, :, lo:lo + BLOCK] = jax.nn.sigmoid(t[2 * proj:])
        return 0

    lax.fori_loop(0, GROUP, one, 0)


def attend(j, lo, rows, heads, head_dim, bias_scr, k_scr, q_scr, v_scr, g_scr, s_scr, w_o):
    proj = heads * head_dim
    q_all = q_scr[j, :, pl.ds(lo, BLOCK)]
    gated = []
    for h in range(heads):
        hs = slice(h * head_dim, (h + 1) * head_dim)
        parts = []
        if h:
            parts.append(jnp.zeros((h * head_dim, BLOCK), BF16))
        parts.append(q_all[hs])
        if h < heads - 1:
            parts.append(jnp.zeros((proj - (h + 1) * head_dim, BLOCK), BF16))
        q_pad = jnp.concatenate(parts, axis=0)
        top = None
        for kc in range(0, rows, BLOCK):
            s = jnp.dot(k_scr[j, kc:kc + BLOCK], q_pad, preferred_element_type=F32) + bias_scr[h, kc:kc + BLOCK, pl.ds(lo, BLOCK)]
            s_scr[h, kc:kc + BLOCK] = s
            part = jnp.max(s.reshape(BLOCK // 8, 8, BLOCK), axis=0)
            top = part if top is None else jnp.maximum(top, part)
        top = jnp.max(top, axis=0, keepdims=True)
        total = None
        acc = None
        for kc in range(0, rows, BLOCK):
            p = jnp.exp(s_scr[h, kc:kc + BLOCK] - top)
            part = jnp.sum(p.reshape(BLOCK // 8, 8, BLOCK), axis=0)
            total = part if total is None else total + part
            o = jnp.dot(v_scr[j, hs, kc:kc + BLOCK], p.astype(BF16), preferred_element_type=F32)
            acc = o if acc is None else acc + o
        total = jnp.sum(total, axis=0, keepdims=True)
        gated.append((g_scr[j, hs, pl.ds(lo, BLOCK)] * (acc / total)).astype(BF16))
    gated = jnp.concatenate(gated, axis=0)
    return lax.dot_general(gated, w_o[...], TN, preferred_element_type=F32)


def attn_kernel(heads, z_ref, bias_ref, fill_ref, gamma_ref, beta_ref, w_k, w_qvg_t, w_o, out_ref,
                a_scr, k_scr, q_scr, v_scr, g_scr, bias_scr, s_scr):
    rows = z_ref.shape[0]
    head_dim = w_k.shape[1] // heads

    @pl.when(pl.program_id(0) == 0)
    def _():
        def one(t, _):
            lo = pl.multiple_of(t * 32, 32)
            for h in range(heads):
                bias_scr[h, pl.ds(lo, 32), :] = bias_ref[h, pl.ds(lo, 32), :].astype(F32) + fill_ref[pl.ds(lo, 32), :]
            return 0
        lax.fori_loop(0, rows // 32, one, 0)

    norm_group(z_ref, gamma_ref[...], beta_ref[...], a_scr)
    project_group(rows, a_scr, w_k, w_qvg_t, k_scr, q_scr, v_scr, g_scr, head_dim)

    def unit(t, _):
        j = lax.rem(t, GROUP)
        lo = pl.multiple_of((t // GROUP) * BLOCK, BLOCK)
        upd = attend(j, lo, rows, heads, head_dim, bias_scr, k_scr, q_scr, v_scr, g_scr, s_scr, w_o)
        a_scr[pl.ds(lo * GROUP + j, BLOCK, stride=GROUP), :] = upd
        return 0

    lax.fori_loop(0, GROUP * (rows // BLOCK), unit, 0)

    def fin(t, _):
        lo = pl.multiple_of(t * 64, 64)
        upd = a_scr[pl.ds(pl.multiple_of(lo * GROUP, 64 * GROUP), 64 * GROUP), :].reshape(64, GROUP, a_scr.shape[1])
        out_ref[pl.ds(lo, 64)] = (z_ref[pl.ds(lo, 64)].astype(F32) + upd).astype(BF16)
        return 0

    lax.fori_loop(0, rows // 64, fin, 0)


def attention(z_t, bias, fill, gamma, beta, w_k, w_qvg_t, w_o):
    rows, cols, chan = z_t.shape
    heads = bias.shape[0]
    proj = w_k.shape[1]
    full = lambda *shape: pl.BlockSpec(shape, lambda g: (0,) * len(shape), pipeline_mode=pl.Buffered(1))
    blk = pl.BlockSpec((rows, GROUP, chan), lambda g: (0, g, 0))
    return pl.pallas_call(
        functools.partial(attn_kernel, heads),
        grid=(cols // GROUP,),
        out_shape=jax.ShapeDtypeStruct(z_t.shape, BF16),
        in_specs=[blk, full(heads, rows, rows), full(rows, 1), full(1, chan), full(1, chan), full(chan, proj),
                  full(3 * proj, chan), full(proj, chan)],
        out_specs=blk,
        scratch_shapes=[
            pltpu.VMEM((rows * GROUP, chan), F32),
            pltpu.VMEM((GROUP, rows, proj), BF16),
            pltpu.VMEM((GROUP, proj, rows), BF16),
            pltpu.VMEM((GROUP, proj, rows), BF16),
            pltpu.VMEM((GROUP, proj, rows), F32),
            pltpu.VMEM((heads, rows, rows), F32),
            pltpu.VMEM((heads, rows, BLOCK), F32),
        ],
        compiler_params=pltpu.CompilerParams(vmem_limit_bytes=58 * 1024 * 1024),
        name="attend",
    )(z_t, bias, fill, gamma, beta, w_k, w_qvg_t, w_o)


def solution(mesh):
    def body(pair_tile, res_mask, ln_gamma, ln_beta, w_q, w_k, w_v, w_b, w_g, w_o):
        block, cols, chan = pair_tile.shape
        z_t = lax.all_to_all(pair_tile, 'row', 1, 0, tiled=True)
        normed = layer_norm(pair_tile.astype(F32), ln_gamma, ln_beta).astype(BF16)
        bias = jnp.einsum('kic,ch->hki', normed, w_b, preferred_element_type=F32).astype(BF16)
        bias = lax.all_gather(bias, 'row', axis=1, tiled=True)
        bias = lax.all_gather(bias, 'col', axis=2, tiled=True)
        fill = jnp.where(res_mask > 0, 0.0, MASK_FILL).astype(F32)[:, None]
        w_qvg_t = jnp.concatenate([w_q.T, w_v.T, w_g.T], axis=0)
        out_t = attention(z_t, bias, fill, ln_gamma[None], ln_beta[None], w_k, w_qvg_t, w_o)
        return lax.all_to_all(out_t, 'row', 0, 1, tiled=True)

    tile_spec = P(('data', 'row'), 'col', None)
    return jax.shard_map(body, mesh=mesh, in_specs=(tile_spec, P('data'), P(), P(), P(), P(), P(), P(), P(), P()), out_specs=tile_spec, check_vma=False)
```

time: 1740 us -> 376 us (0.22)
  waiting for transfers between devices: 947 us -> 78.4 us
  matrix products: 396 us -> 8.64 us
  Pallas kernels: 0 us -> 168 us
  other arithmetic: 176 us -> 11.4 us
  local copies, waits for them, and re-layouts: 167 us -> 31.4 us
  blocking collectives: 15.1 us -> 58.8 us
  starting transfers between devices: 23.4 us -> 5.08 us
    ppermute x7 -> x0, waiting for transfers between devices: 947 us -> none  [shift_step(): kv_blk = lax.ppermute(kv_blk, 'row', next_hop)]
    dot_general x20 -> x1, matrix products: 396 us -> 8.64 us  [body(): jnp.einsum('kic,ch->hki', normed, w_b, preferred_element_type=F32)]
    pallas_call x0 -> x1, Pallas kernels: none -> 168 us  [attention(): pl.pallas_call(functools.partial(attn_kernel, heads), grid=(cols // GROUP...]
    reduce_sum x10 -> x2, other arithmetic: 165 us -> 10.7 us  [the longest x1 6.42 us: layer_norm(): variance = jnp.mean(centred * centred, axis=-1, keepdims=True)]
    while x15 -> x0, local copies, waits for them, and re-layouts: 108 us -> none
    all_to_all x0 -> x1, blocking collectives: none -> 58.8 us  [body(): return lax.all_to_all(out_t, 'row', 0, 1, tiled=True)]
    all_to_all x1, waiting for transfers between devices: 0.01 us -> 52.2 us  [body(): z_t = lax.all_to_all(pair_tile, 'row', 1, 0, tiled=True)]
    squeeze x3 -> x0, local copies, waits for them, and re-layouts: 37.5 us -> none  [the longest x2 24.1 us: attend_block(): kv_blk[1]]
  transfers between devices with their start and end apart: 8 -> 3, of which waited for: 7 -> 2; matrix products, arithmetic and copies ran while one was open for 6% -> 4% of each run, Pallas kernels for 0% -> 0%
where the time goes in v1:
time: 376 us; the launch traced here: 375 us
  Pallas kernels  168 us (45%)
  waiting for transfers between devices  78.4 us (21%)
  blocking collectives  58.8 us (16%)
  local copies, waits for them, and re-layouts  31.4 us (8%)
  between operations  13.6 us (4%)
  other arithmetic  11.4 us (3%)
  matrix products  8.64 us (2%)
  starting transfers between devices  5.08 us (1%)
    pallas_call x1, Pallas kernels, attention(): pl.pallas_call(functools.partial(attn_kernel, heads), grid=(cols // GROUP...  168 us
    all_to_all x1, blocking collectives, body(): return lax.all_to_all(out_t, 'row', 0, 1, tiled=True)  58.8 us
    all_to_all x1, waiting for transfers between devices, body(): z_t = lax.all_to_all(pair_tile, 'row', 1, 0, tiled=True)  52.2 us
    all_gather x1, waiting for transfers between devices, body(): bias = lax.all_gather(bias, 'row', axis=1, tiled=True)  26.1 us
    dot_general x1, matrix products, body(): jnp.einsum('kic,ch->hki', normed, w_b, preferred_element_type=F32)  8.64 us
    all_gather x1, local copies, waits for them, and re-layouts, body(): bias = lax.all_gather(bias, 'col', axis=2, tiled=True)  8.46 us
    unnamed x20, local copies, waits for them, and re-layouts  7.93 us
  transfers between devices with their start and end apart: 3, of which 2 were waited for; matrix products, arithmetic and copies ran while one was open for 4% of the time, Pallas kernels for 0%

profile of v1, /device:TPU:97, one launch (start us, length us, event | category | flops | bytes accessed | tf_op | source)
XLA Modules:
  0.0 375.1 jit_solution(11305790687666996855)
XLA Ops:
  6.5 0.0 copy-start
  6.6 0.0 copy-start.7
  6.6 0.0 copy-start.6
  6.6 0.0 all-gather.3.cloned.1.call-start
  6.6 0.0 copy-start.1
  6.6 4.3 %convert_reduce_fusion = f32[96,192]{1,0:T(8,128)S(1)} fusion(bf16[96,192,128]{2,1,0:T(8,128)(2,1)} %param.10), kind=kLoop, calls=%fused_computation.1 | loop fusion | flops 4700160 | bytes 4792320 | tf_op jit(solution)/shard_map/reduce_sum | solution.py:21
  10.9 0.0 copy-done.1
  10.9 6.4 %fusion.2 = f32[96,192]{1,0:T(8,128)S(1)} fusion(bf16[96,192,128]{2,1,0:T(8,128)(2,1)S(1)} %copy-done.1, f32[96,192]{1,0:T(8,128)S(1)} %broadcast_multiply_fusion), kind=kLoop, calls=%fused_computation.4 | loop fusion | flops 9418752 | bytes 4866048 | tf_op jit(solution)/shard_map/reduce_sum | solution.py:23
  17.3 0.0 copy-done
  17.3 0.0 copy-done.7
  17.4 0.0 copy-done.6
  17.4 8.6 %fusion.11 = bf16[4,96,192]{2,0,1:T(4,128)(2,1)} fusion(bf16[96,192,128]{2,1,0:T(8,128)(2,1)S(1)} %copy-done.1, f32[128]{0:T(128)S(1)} %copy-done.6, f32[128]{0:T(128)S(1)} %copy-done.7, f32[96,192]{1,0:T(8,128)S(1)} %add_rsqrt_fusion, f32[96,192]{1,0:T(8,128)S(1)} %broadcast_multiply_fusion, bf16[128,4]{0,1:T(4,128)(2,1)S(1)} %copy-done), kind=kOutput, calls=%fused_computation.10 | convolution fusion | flops 33103872 | bytes 5015552 | tf_op jit(solution)/shard_map/kic,ch->hki/dot_general | solution.py:156
  26.0 0.1 all-gather.3.cloned.1.call-update
  26.1 0.1 all-gather.5.cloned.1.call-start
  26.1 26.1 %all-gather.3.cloned.1.call-done = bf16[4,768,192]{2,0,1:T(4,128)(2,1)} async-done(((bf16[4,96,192]{2,0,1:T(4,128)(2,1)}), bf16[4,768,192]{2,0,1:T(4,128)(2,1)}) %all-gather.3.cloned.1.call-update) | async-done | bytes 1179664 | tf_op jit(solution)/shard_map/all_gather | solution.py:157
  52.3 4.2 %copy.35 = bf16[4,768,192]{1,0,2:T(4,128)(2,1)} copy(bf16[4,768,192]{2,0,1:T(4,128)(2,1)} %all-gather.3.cloned.1.call-done) | data formatting | bytes 2359296 | tf_op jit(solution)/shard_map/all_gather | solution.py:157
  56.4 0.1 all-gather.5.cloned.1.call-update
  56.5 7.6 %copy.33 = bf16[96,192,128]{2,0,1:T(8,128)(2,1)} copy(bf16[96,192,128]{2,1,0:T(8,128)(2,1)} %param.10) | data formatting | bytes 9437184 | tf_op args[0]
  64.1 0.0 copy-start.5
  64.1 0.0 copy-start.2
  64.1 0.0 copy-start.3
  64.1 0.0 copy-start.4
  64.1 5.0 %all-to-all-start = ((bf16[96,192,128]{2,0,1:T(8,128)(2,1)}), bf16[96,192,128]{2,0,1:T(8,128)(2,1)}, u32[]{:S(2)}, u32[]{:S(2)}) async-start(bf16[96,192,128]{2,0,1:T(8,128)(2,1)} %copy.33), calls=%async_computation | async-start | bytes 9437184 | tf_op jit(solution)/shard_map/all_to_all | solution.py:154
  69.1 0.0 copy-done.5
  69.1 0.9 broadcast_in_dim.26.fill_ref
  70.0 0.0 copy-done.2
  70.0 0.1 copy.36
  70.1 0.0 copy-done.3
  70.2 0.1 copy.37
  70.3 0.0 copy-done.4
  70.3 0.1 copy.38
  70.4 0.7 pad_maximum_fusion.w_qvg_t
  71.1 52.2 %all-to-all-done = bf16[96,192,128]{2,0,1:T(8,128)(2,1)} async-done(((bf16[96,192,128]{2,0,1:T(8,128)(2,1)}), bf16[96,192,128]{2,0,1:T(8,128)(2,1)}, u32[]{:S(2)}, u32[]{:S(2)}) %all-to-all-start) | async-done | bytes 4718624 | tf_op jit(solution)/shard_map/all_to_all | solution.py:154
  123.3 6.3 %copy.34 = bf16[96,8,24,128]{3,2,0,1:T(8,128)(2,1)} copy(bf16[96,8,24,128]{3,0,2,1:T(8,128)(2,1)} %bitcast) | data formatting | bytes 9437184 | tf_op jit(solution)/shard_map/all_to_all | solution.py:154
  129.6 0.0 all-gather.5.cloned.1.call-done
  129.6 8.5 %copy.39.bias_ref = bf16[4,768,768]{2,1,0:T(8,128)(2,1)} copy(bf16[4,768,768]{1,0,2:T(4,128)(2,1)} %all-gather.5.cloned.1.call-done) | data formatting | bytes 9437184 | tf_op jit(solution)/shard_map/all_gather | solution.py:158
  138.1 167.8 %attend.1 = bf16[768,24,128]{2,1,0:T(8,128)(2,1)} custom-call(bf16[768,24,128]{2,1,0:T(8,128)(2,1)} %bitcast.19, bf16[4,768,768]{2,1,0:T(8,128)(2,1)} %copy.39.bias_ref, f32[768,1]{1,0:T(8,128)} %broadcast_in_dim.26.fill_ref, f32[1,128]{1,0:T(1,128)} %bitcast.24, f32[1,128]{1,0:T(1,128)} %bitcast.23, bf16[128,128]{1,0:T(8,128)(2,1)} %w_k.1, ...), custom_call_target="tpu_custom_call" | custom-call | tf_op jit(solution)/shard_map/attend/pallas_call | solution.py:130
  305.9 58.8 %all_to_all.36 = bf16[768,24,128]{2,1,0:T(8,128)(2,1)S(1)} all-to-all(bf16[768,24,128]{2,1,0:T(8,128)(2,1)} %attend.1), channel_id=1, replica_groups=mesh['data'=1,'col'=4,'row'=8] {'row'}, dimensions={0} | all-to-all | bytes 9437184 | tf_op jit(solution)/shard_map/all_to_all | solution.py:162
  364.7 3.5 copy.41
  (3 shorter events, 0.0 us)
Async XLA Ops:
  6.5 10.8 %copy-start = (bf16[128,4]{0,1:T(4,128)(2,1)S(1)}, bf16[128,4]{0,1:T(4,128)(2,1)}, u32[]{:S(2)}) copy-start(bf16[128,4]{0,1:T(4,128)(2,1)} %param.17) | copy-start | bytes 3076
  6.6 10.8 %copy-start.7 = (f32[128]{0:T(128)S(1)}, f32[128]{0:T(128)}, u32[]{:S(2)}) copy-start(f32[128]{0:T(128)} %param.12) | copy-start | bytes 1540
  6.6 10.8 %copy-start.6 = (f32[128]{0:T(128)S(1)}, f32[128]{0:T(128)}, u32[]{:S(2)}) copy-start(f32[128]{0:T(128)} %param.13) | copy-start | bytes 1540
  6.6 45.7 %all-gather.3.cloned.1.call-start = ((), (), s32[]{:S(2)}) async-start(), calls=%async_computation.2 | async-start | bytes 1769472 | tf_op jit(solution)/shard_map/all_gather | solution.py:157
  6.6 4.3 %copy-start.1 = (bf16[96,192,128]{2,1,0:T(8,128)(2,1)S(1)}, bf16[96,192,128]{2,1,0:T(8,128)(2,1)}, u32[]{:S(2)}) copy-start(bf16[96,192,128]{2,1,0:T(8,128)(2,1)} %param.10) | copy-start | bytes 14155780
  26.1 103.6 %all-gather.5.cloned.1.call-start = ((), (), s32[]{:S(2)}) async-start(), calls=%async_computation.3 | async-start | bytes 5898240 | tf_op jit(solution)/shard_map/all_gather | solution.py:158
  64.1 5.0 %copy-start.5 = (s32[768]{0:T(1024)S(1)}, s32[768]{0:T(1024)}, u32[]{:S(2)}) copy-start(s32[768]{0:T(1024)} %param.11) | copy-start | bytes 9220
  64.1 6.0 %copy-start.2 = (bf16[128,128]{1,0:T(8,128)(2,1)S(1)}, bf16[128,128]{1,0:T(8,128)(2,1)}, u32[]{:S(2)}) copy-start(bf16[128,128]{1,0:T(8,128)(2,1)} %param.14) | copy-start | bytes 98308
  64.1 6.1 %copy-start.3 = (bf16[128,128]{1,0:T(8,128)(2,1)S(1)}, bf16[128,128]{1,0:T(8,128)(2,1)}, u32[]{:S(2)}) copy-start(bf16[128,128]{1,0:T(8,128)(2,1)} %param.16) | copy-start | bytes 98308
  64.1 6.2 %copy-start.4 = (bf16[128,128]{1,0:T(8,128)(2,1)S(1)}, bf16[128,128]{1,0:T(8,128)(2,1)}, u32[]{:S(2)}) copy-start(bf16[128,128]{1,0:T(8,128)(2,1)} %param.18) | copy-start | bytes 98308
  64.1 59.2 %all-to-all-start = ((bf16[96,192,128]{2,0,1:T(8,128)(2,1)}), bf16[96,192,128]{2,0,1:T(8,128)(2,1)}, u32[]{:S(2)}, u32[]{:S(2)}) async-start(bf16[96,192,128]{2,0,1:T(8,128)(2,1)} %copy.33), calls=%async_computation | async-start | bytes 9437184 | tf_op jit(solution)/shard_map/all_to_all | solution.py:154
Sparse Core Ops, SparseCore 0:
  26.2 26.0 all-gather.2
  56.6 49.4 all-gather.4

commit v2 on v1

--- a/solution.py
+++ b/solution.py
@@ -44,50 +44,82 @@
         k_scr[j] = jnp.dot(a, w_k[...], preferred_element_type=F32).astype(BF16)
         for lo in range(0, rows, BLOCK):
             t = lax.dot_general(w_qvg_t[...], a[lo:lo + BLOCK], NT, preferred_element_type=F32)
-            q_scr[j, :, lo:lo + BLOCK] = (t[:proj] * (1.0 / math.sqrt(head_dim))).astype(BF16)
-            v_scr[j, :, lo:lo + BLOCK] = t[proj:2 * proj].astype(BF16)
-            g_scr[j, :, lo:lo + BLOCK] = jax.nn.sigmoid(t[2 * proj:])
+            for h in range(proj // head_dim):
+                hs = slice(h * head_dim, (h + 1) * head_dim)
+                q_scr[j, h, hs, lo:lo + BLOCK] = (t[hs] * (1.0 / math.sqrt(head_dim))).astype(BF16)
+                v_scr[j, h, :, lo:lo + BLOCK] = t[proj:2 * proj][hs].astype(BF16)
+                g_scr[j, h, :, lo:lo + BLOCK] = jax.nn.sigmoid(t[2 * proj:][hs])
         return 0
 
     lax.fori_loop(0, GROUP, one, 0)
 
 
-def attend(j, lo, rows, heads, head_dim, bias_scr, k_scr, q_scr, v_scr, g_scr, s_scr, w_o):
-    proj = heads * head_dim
-    q_all = q_scr[j, :, pl.ds(lo, BLOCK)]
-    gated = []
-    for h in range(heads):
-        hs = slice(h * head_dim, (h + 1) * head_dim)
-        parts = []
-        if h:
-            parts.append(jnp.zeros((h * head_dim, BLOCK), BF16))
-        parts.append(q_all[hs])
-        if h < heads - 1:
-            parts.append(jnp.zeros((proj - (h + 1) * head_dim, BLOCK), BF16))
-        q_pad = jnp.concatenate(parts, axis=0)
-        top = None
-        for kc in range(0, rows, BLOCK):
-            s = jnp.dot(k_scr[j, kc:kc + BLOCK], q_pad, preferred_element_type=F32) + bias_scr[h, kc:kc + BLOCK, pl.ds(lo, BLOCK)]
-            s_scr[h, kc:kc + BLOCK] = s
-            part = jnp.max(s.reshape(BLOCK // 8, 8, BLOCK), axis=0)
-            top = part if top is None else jnp.maximum(top, part)
-        top = jnp.max(top, axis=0, keepdims=True)
-        total = None
-        acc = None
-        for kc in range(0, rows, BLOCK):
-            p = jnp.exp(s_scr[h, kc:kc + BLOCK] - top)
-            part = jnp.sum(p.reshape(BLOCK // 8, 8, BLOCK), axis=0)
-            total = part if total is None else total + part
-            o = jnp.dot(v_scr[j, hs, kc:kc + BLOCK], p.astype(BF16), preferred_element_type=F32)
-            acc = o if acc is None else acc + o
-        total = jnp.sum(total, axis=0, keepdims=True)
-        gated.append((g_scr[j, hs, pl.ds(lo, BLOCK)] * (acc / total)).astype(BF16))
-    gated = jnp.concatenate(gated, axis=0)
-    return lax.dot_general(gated, w_o[...], TN, preferred_element_type=F32)
+KC = 256
+HB = 4
+
+
+def score_chunk(j, h, lo, kc, bias_scr, k_scr, q_scr):
+    q_pad = q_scr[j, h, :, pl.ds(lo, BLOCK)]
+    return jnp.dot(k_scr[j, kc:kc + KC], q_pad, preferred_element_type=F32) + bias_scr[h, kc:kc + KC, pl.ds(lo, BLOCK)]
+
+
+def fold8(x, op):
+    return op(x.reshape(x.shape[0] // 8, 8, x.shape[1]), axis=0)
+
+
+def scores(j, h, hb, lo, rows, bias_scr, k_scr, q_scr, s_scr, top_scr):
+    top = None
+    for kc in range(0, rows, KC):
+        s = score_chunk(j, h, lo, kc, bias_scr, k_scr, q_scr)
+        s_scr[hb, kc:kc + KC] = s
+        part = fold8(s, jnp.max)
+        top = part if top is None else jnp.maximum(top, part)
+    top_scr[hb] = jnp.max(top, axis=0, keepdims=True)
+
+
+def soft_and_next(cur, nxt, hb, rows, bias_scr, k_scr, q_scr, v_scr, g_scr, s_scr, top_scr, o_scr):
+    j, h, lo = cur
+    nj, nh, nlo = nxt
+    top = top_scr[hb]
+    total = acc = ntop = None
+    for kc in range(0, rows, KC):
+        p = jnp.exp(s_scr[hb, kc:kc + KC] - top)
+        part = fold8(p, jnp.sum)
+        total = part if total is None else total + part
+        o = jnp.dot(v_scr[j, h, :, kc:kc + KC], p.astype(BF16), preferred_element_type=F32)
+        acc = o if acc is None else acc + o
+        s = score_chunk(nj, nh, nlo, kc, bias_scr, k_scr, q_scr)
+        s_scr[hb, kc:kc + KC] = s
+        part = fold8(s, jnp.max)
+        ntop = part if ntop is None else jnp.maximum(ntop, part)
+    top_scr[hb] = jnp.max(ntop, axis=0, keepdims=True)
+    total = jnp.sum(total, axis=0, keepdims=True)
+    o_scr[j, h, :, pl.ds(lo, BLOCK)] = (g_scr[j, h, :, pl.ds(lo, BLOCK)] * (acc / total)).astype(BF16)
+
+
+def attend_all(units, rows, heads, bias_scr, k_scr, q_scr, v_scr, g_scr, s_scr, top_scr, o_scr):
+    per = heads // HB
+
+    def where(t, hb):
+        u = t // per
+        return lax.rem(u, GROUP), lax.rem(t, per) * HB + hb, pl.multiple_of((u // GROUP) * BLOCK, BLOCK)
+
+    n = units * per
+    for hb in range(HB):
+        j, h, lo = where(0, hb)
+        scores(j, h, hb, lo, rows, bias_scr, k_scr, q_scr, s_scr, top_scr)
+
+    def one(t, _):
+        nt = jnp.minimum(t + 1, n - 1)
+        for hb in range(HB):
+            soft_and_next(where(t, hb), where(nt, hb), hb, rows, bias_scr, k_scr, q_scr, v_scr, g_scr, s_scr, top_scr, o_scr)
+        return 0
+
+    lax.fori_loop(0, n, one, 0)
 
 
 def attn_kernel(heads, z_ref, bias_ref, fill_ref, gamma_ref, beta_ref, w_k, w_qvg_t, w_o, out_ref,
-                a_scr, k_scr, q_scr, v_scr, g_scr, bias_scr, s_scr):
+                a_scr, k_scr, q_scr, v_scr, g_scr, bias_scr, s_scr, top_scr, o_scr):
     rows = z_ref.shape[0]
     head_dim = w_k.shape[1] // heads
 
@@ -99,18 +131,21 @@
                 bias_scr[h, pl.ds(lo, 32), :] = bias_ref[h, pl.ds(lo, 32), :].astype(F32) + fill_ref[pl.ds(lo, 32), :]
             return 0
         lax.fori_loop(0, rows // 32, one, 0)
+        q_scr[...] = jnp.zeros_like(q_scr)
 
     norm_group(z_ref, gamma_ref[...], beta_ref[...], a_scr)
     project_group(rows, a_scr, w_k, w_qvg_t, k_scr, q_scr, v_scr, g_scr, head_dim)
 
-    def unit(t, _):
-        j = lax.rem(t, GROUP)
-        lo = pl.multiple_of((t // GROUP) * BLOCK, BLOCK)
-        upd = attend(j, lo, rows, heads, head_dim, bias_scr, k_scr, q_scr, v_scr, g_scr, s_scr, w_o)
-        a_scr[pl.ds(lo * GROUP + j, BLOCK, stride=GROUP), :] = upd
-        return 0
-
-    lax.fori_loop(0, GROUP * (rows // BLOCK), unit, 0)
+    attend_all(GROUP * (rows // BLOCK), rows, heads, bias_scr, k_scr, q_scr, v_scr, g_scr, s_scr, top_scr, o_scr)
+
+    def unit(j, _):
+        for lo in range(0, rows, BLOCK):
+            gated = o_scr[j, :, :, lo:lo + BLOCK].reshape(heads * head_dim, BLOCK)
+            upd = lax.dot_general(gated, w_o[...], TN, preferred_element_type=F32)
+            a_scr[pl.ds(lo * GROUP + j, BLOCK, stride=GROUP), :] = upd
+        return 0
+
+    lax.fori_loop(0, GROUP, unit, 0)
 
     def fin(t, _):
         lo = pl.multiple_of(t * 64, 64)
@@ -137,11 +172,13 @@
         scratch_shapes=[
             pltpu.VMEM((rows * GROUP, chan), F32),
             pltpu.VMEM((GROUP, rows, proj), BF16),
-            pltpu.VMEM((GROUP, proj, rows), BF16),
-            pltpu.VMEM((GROUP, proj, rows), BF16),
-            pltpu.VMEM((GROUP, proj, rows), F32),
+            pltpu.VMEM((GROUP, heads, proj, rows), BF16),
+            pltpu.VMEM((GROUP, heads, proj // heads, rows), BF16),
+            pltpu.VMEM((GROUP, heads, proj // heads, rows), F32),
             pltpu.VMEM((heads, rows, rows), F32),
-            pltpu.VMEM((heads, rows, BLOCK), F32),
+            pltpu.VMEM((HB, rows, BLOCK), F32),
+            pltpu.VMEM((HB, 1, BLOCK), F32),
+            pltpu.VMEM((GROUP, heads, proj // heads, rows), BF16),
         ],
         compiler_params=pltpu.CompilerParams(vmem_limit_bytes=58 * 1024 * 1024),
         name="attend",

time: 376 us -> 307 us (0.82)
  Pallas kernels: 168 us -> 98.9 us
    pallas_call x1, Pallas kernels: 168 us -> 98.9 us  [attention(): pl.pallas_call(functools.partial(attn_kernel, heads), grid=(cols // GROUP...]
  transfers between devices with their start and end apart: 3 -> 3, of which waited for: 2 -> 2; matrix products, arithmetic and copies ran while one was open for 4% -> 5% of each run, Pallas kernels for 0% -> 0%
where the time goes in v2:
time: 307 us; the launch traced here: 306 us
  Pallas kernels  98.9 us (32%)
  waiting for transfers between devices  78.4 us (26%)
  blocking collectives  58.8 us (19%)
  local copies, waits for them, and re-layouts  31.4 us (10%)
  between operations  13.6 us (4%)
  other arithmetic  11.4 us (4%)
  matrix products  8.64 us (3%)
  starting transfers between devices  5.08 us (2%)
    pallas_call x1, Pallas kernels, attention(): pl.pallas_call(functools.partial(attn_kernel, heads), grid=(cols // GROUP...  98.9 us
    all_to_all x1, blocking collectives, body(): return lax.all_to_all(out_t, 'row', 0, 1, tiled=True)  58.8 us
    all_to_all x1, waiting for transfers between devices, body(): z_t = lax.all_to_all(pair_tile, 'row', 1, 0, tiled=True)  52.2 us
    all_gather x1, waiting for transfers between devices, body(): bias = lax.all_gather(bias, 'row', axis=1, tiled=True)  26.1 us
    dot_general x1, matrix products, body(): jnp.einsum('kic,ch->hki', normed, w_b, preferred_element_type=F32)  8.64 us
    all_gather x1, local copies, waits for them, and re-layouts, body(): bias = lax.all_gather(bias, 'col', axis=2, tiled=True)  8.46 us
    unnamed x20, local copies, waits for them, and re-layouts  7.93 us
    reduce_sum x1, other arithmetic, layer_norm(): variance = jnp.mean(centred * centred, axis=-1, keepdims=True)  6.42 us
  transfers between devices with their start and end apart: 3, of which 2 were waited for; matrix products, arithmetic and copies ran while one was open for 5% of the time, Pallas kernels for 0%

profile of v2, /device:TPU:97, one launch (start us, length us, event | category | flops | bytes accessed | tf_op | source)
XLA Modules:
  0.0 306.2 jit_solution(13585491105469882171)
XLA Ops:
  6.5 0.0 copy-start
  6.6 0.0 copy-start.7
  6.6 0.0 copy-start.6
  6.6 0.0 all-gather.3.cloned.1.call-start
  6.6 0.0 copy-start.1
  6.6 4.3 %convert_reduce_fusion = f32[96,192]{1,0:T(8,128)S(1)} fusion(bf16[96,192,128]{2,1,0:T(8,128)(2,1)} %param.10), kind=kLoop, calls=%fused_computation.1 | loop fusion | flops 4700160 | bytes 4792320 | tf_op jit(solution)/shard_map/reduce_sum | solution.py:21
  10.9 0.0 copy-done.1
  10.9 6.4 %fusion.2 = f32[96,192]{1,0:T(8,128)S(1)} fusion(bf16[96,192,128]{2,1,0:T(8,128)(2,1)S(1)} %copy-done.1, f32[96,192]{1,0:T(8,128)S(1)} %broadcast_multiply_fusion), kind=kLoop, calls=%fused_computation.4 | loop fusion | flops 9418752 | bytes 4866048 | tf_op jit(solution)/shard_map/reduce_sum | solution.py:23
  17.3 0.0 copy-done
  17.3 0.0 copy-done.7
  17.4 0.0 copy-done.6
  17.4 8.6 %fusion.11 = bf16[4,96,192]{2,0,1:T(4,128)(2,1)} fusion(bf16[96,192,128]{2,1,0:T(8,128)(2,1)S(1)} %copy-done.1, f32[128]{0:T(128)S(1)} %copy-done.6, f32[128]{0:T(128)S(1)} %copy-done.7, f32[96,192]{1,0:T(8,128)S(1)} %add_rsqrt_fusion, f32[96,192]{1,0:T(8,128)S(1)} %broadcast_multiply_fusion, bf16[128,4]{0,1:T(4,128)(2,1)S(1)} %copy-done), kind=kOutput, calls=%fused_computation.10 | convolution fusion | flops 33103872 | bytes 5015552 | tf_op jit(solution)/shard_map/kic,ch->hki/dot_general | solution.py:193
  26.0 0.1 all-gather.3.cloned.1.call-update
  26.1 0.1 all-gather.5.cloned.1.call-start
  26.1 26.1 %all-gather.3.cloned.1.call-done = bf16[4,768,192]{2,0,1:T(4,128)(2,1)} async-done(((bf16[4,96,192]{2,0,1:T(4,128)(2,1)}), bf16[4,768,192]{2,0,1:T(4,128)(2,1)}) %all-gather.3.cloned.1.call-update) | async-done | bytes 1179664 | tf_op jit(solution)/shard_map/all_gather | solution.py:194
  52.3 4.2 %copy.35 = bf16[4,768,192]{1,0,2:T(4,128)(2,1)} copy(bf16[4,768,192]{2,0,1:T(4,128)(2,1)} %all-gather.3.cloned.1.call-done) | data formatting | bytes 2359296 | tf_op jit(solution)/shard_map/all_gather | solution.py:194
  56.4 0.1 all-gather.5.cloned.1.call-update
  56.5 7.6 %copy.33 = bf16[96,192,128]{2,0,1:T(8,128)(2,1)} copy(bf16[96,192,128]{2,1,0:T(8,128)(2,1)} %param.10) | data formatting | bytes 9437184 | tf_op args[0]
  64.1 0.0 copy-start.5
  64.1 0.0 copy-start.2
  64.1 0.0 copy-start.3
  64.1 0.0 copy-start.4
  64.1 5.0 %all-to-all-start = ((bf16[96,192,128]{2,0,1:T(8,128)(2,1)}), bf16[96,192,128]{2,0,1:T(8,128)(2,1)}, u32[]{:S(2)}, u32[]{:S(2)}) async-start(bf16[96,192,128]{2,0,1:T(8,128)(2,1)} %copy.33), calls=%async_computation | async-start | bytes 9437184 | tf_op jit(solution)/shard_map/all_to_all | solution.py:191
  69.1 0.0 copy-done.5
  69.1 0.9 broadcast_in_dim.26.fill_ref
  70.0 0.0 copy-done.2
  70.0 0.1 copy.36
  70.1 0.0 copy-done.3
  70.2 0.1 copy.37
  70.3 0.0 copy-done.4
  70.3 0.1 copy.38
  70.4 0.7 pad_maximum_fusion.w_qvg_t
  71.1 52.2 %all-to-all-done = bf16[96,192,128]{2,0,1:T(8,128)(2,1)} async-done(((bf16[96,192,128]{2,0,1:T(8,128)(2,1)}), bf16[96,192,128]{2,0,1:T(8,128)(2,1)}, u32[]{:S(2)}, u32[]{:S(2)}) %all-to-all-start) | async-done | bytes 4718624 | tf_op jit(solution)/shard_map/all_to_all | solution.py:191
  123.3 6.3 %copy.34 = bf16[96,8,24,128]{3,2,0,1:T(8,128)(2,1)} copy(bf16[96,8,24,128]{3,0,2,1:T(8,128)(2,1)} %bitcast) | data formatting | bytes 9437184 | tf_op jit(solution)/shard_map/all_to_all | solution.py:191
  129.6 0.0 all-gather.5.cloned.1.call-done
  129.6 8.5 %copy.39.bias_ref = bf16[4,768,768]{2,1,0:T(8,128)(2,1)} copy(bf16[4,768,768]{1,0,2:T(4,128)(2,1)} %all-gather.5.cloned.1.call-done) | data formatting | bytes 9437184 | tf_op jit(solution)/shard_map/all_gather | solution.py:195
  138.1 98.9 %attend.1 = bf16[768,24,128]{2,1,0:T(8,128)(2,1)} custom-call(bf16[768,24,128]{2,1,0:T(8,128)(2,1)} %bitcast.19, bf16[4,768,768]{2,1,0:T(8,128)(2,1)} %copy.39.bias_ref, f32[768,1]{1,0:T(8,128)} %broadcast_in_dim.26.fill_ref, f32[1,128]{1,0:T(1,128)} %bitcast.24, f32[1,128]{1,0:T(1,128)} %bitcast.23, bf16[128,128]{1,0:T(8,128)(2,1)} %w_k.1, ...), custom_call_target="tpu_custom_call" | custom-call | tf_op jit(solution)/shard_map/attend/pallas_call | solution.py:165
  237.0 58.8 %all_to_all.36 = bf16[768,24,128]{2,1,0:T(8,128)(2,1)S(1)} all-to-all(bf16[768,24,128]{2,1,0:T(8,128)(2,1)} %attend.1), channel_id=1, replica_groups=mesh['data'=1,'col'=4,'row'=8] {'row'}, dimensions={0} | all-to-all | bytes 9437184 | tf_op jit(solution)/shard_map/all_to_all | solution.py:199
  295.8 3.5 %copy.41 = bf16[96,8,24,128]{3,2,1,0:T(8,128)(2,1)} copy(bf16[96,8,24,128]{3,2,0,1:T(8,128)(2,1)S(1)} %bitcast.18) | data formatting | bytes 9437184 | tf_op jit(solution)/shard_map/all_to_all | solution.py:199
  (3 shorter events, 0.0 us)
Async XLA Ops:
  6.5 10.8 %copy-start = (bf16[128,4]{0,1:T(4,128)(2,1)S(1)}, bf16[128,4]{0,1:T(4,128)(2,1)}, u32[]{:S(2)}) copy-start(bf16[128,4]{0,1:T(4,128)(2,1)} %param.17) | copy-start | bytes 3076
  6.6 10.8 %copy-start.7 = (f32[128]{0:T(128)S(1)}, f32[128]{0:T(128)}, u32[]{:S(2)}) copy-start(f32[128]{0:T(128)} %param.12) | copy-start | bytes 1540
  6.6 10.8 %copy-start.6 = (f32[128]{0:T(128)S(1)}, f32[128]{0:T(128)}, u32[]{:S(2)}) copy-start(f32[128]{0:T(128)} %param.13) | copy-start | bytes 1540
  6.6 45.7 %all-gather.3.cloned.1.call-start = ((), (), s32[]{:S(2)}) async-start(), calls=%async_computation.2 | async-start | bytes 1769472 | tf_op jit(solution)/shard_map/all_gather | solution.py:194
  6.6 4.3 %copy-start.1 = (bf16[96,192,128]{2,1,0:T(8,128)(2,1)S(1)}, bf16[96,192,128]{2,1,0:T(8,128)(2,1)}, u32[]{:S(2)}) copy-start(bf16[96,192,128]{2,1,0:T(8,128)(2,1)} %param.10) | copy-start | bytes 14155780
  26.1 103.6 %all-gather.5.cloned.1.call-start = ((), (), s32[]{:S(2)}) async-start(), calls=%async_computation.3 | async-start | bytes 5898240 | tf_op jit(solution)/shard_map/all_gather | solution.py:195
  64.1 5.0 %copy-start.5 = (s32[768]{0:T(1024)S(1)}, s32[768]{0:T(1024)}, u32[]{:S(2)}) copy-start(s32[768]{0:T(1024)} %param.11) | copy-start | bytes 9220
  64.1 6.0 %copy-start.2 = (bf16[128,128]{1,0:T(8,128)(2,1)S(1)}, bf16[128,128]{1,0:T(8,128)(2,1)}, u32[]{:S(2)}) copy-start(bf16[128,128]{1,0:T(8,128)(2,1)} %param.14) | copy-start | bytes 98308
  64.1 6.1 %copy-start.3 = (bf16[128,128]{1,0:T(8,128)(2,1)S(1)}, bf16[128,128]{1,0:T(8,128)(2,1)}, u32[]{:S(2)}) copy-start(bf16[128,128]{1,0:T(8,128)(2,1)} %param.16) | copy-start | bytes 98308
  64.1 6.2 %copy-start.4 = (bf16[128,128]{1,0:T(8,128)(2,1)S(1)}, bf16[128,128]{1,0:T(8,128)(2,1)}, u32[]{:S(2)}) copy-start(bf16[128,128]{1,0:T(8,128)(2,1)} %param.18) | copy-start | bytes 98308
  64.1 59.2 %all-to-all-start = ((bf16[96,192,128]{2,0,1:T(8,128)(2,1)}), bf16[96,192,128]{2,0,1:T(8,128)(2,1)}, u32[]{:S(2)}, u32[]{:S(2)}) async-start(bf16[96,192,128]{2,0,1:T(8,128)(2,1)} %copy.33), calls=%async_computation | async-start | bytes 9437184 | tf_op jit(solution)/shard_map/all_to_all | solution.py:191
Sparse Core Ops, SparseCore 0:
  26.2 26.0 all-gather.2
  56.6 49.4 all-gather.4

commit v3 on v2

v3 whole, which is shorter than its diff:
```python
import functools
import math
import jax
import jax.numpy as jnp
from jax import lax
from jax.experimental import pallas as pl
from jax.experimental.pallas import tpu as pltpu
from jax.sharding import PartitionSpec as P

LN_EPS = 1e-5
MASK_FILL = -1e9
GROUP = 8
BLOCK = 256
PIECE = 32
KC = 256
LANES = 128
HALF = 64
F32 = jnp.float32
BF16 = jnp.bfloat16
NT = (((1,), (1,)), ((), ()))
TN = (((0,), (0,)), ((), ()))
MESH = pl.DeviceIdType.MESH


def layer_norm(z, gamma, beta):
    mean = jnp.mean(z, axis=-1, keepdims=True)
    centred = z - mean
    variance = jnp.mean(centred * centred, axis=-1, keepdims=True)
    return centred * lax.rsqrt(variance + LN_EPS) * gamma + beta


def norm_group(zin, c, gamma, beta, a_scr, step=64):
    rows = zin.shape[1]

    def one(t, _):
        lo = pl.multiple_of(t * step, step)
        a = layer_norm(zin[c, pl.ds(lo, step)].astype(F32), gamma, beta)
        a_scr[pl.ds(pl.multiple_of(lo * GROUP, step * GROUP), step * GROUP), :] = a.reshape(step * GROUP, a.shape[-1])
        return 0

    lax.fori_loop(0, rows // step, one, 0)


def project_group(rows, a_scr, w_k, w_qvg_t, k_scr, q_scr, v_scr, g_scr, head_dim):
    proj = w_k.shape[1]

    def one(j, _):
        a = a_scr[pl.ds(j, rows, stride=GROUP), :].astype(BF16)
        k_scr[j] = jnp.dot(a, w_k[...], preferred_element_type=F32).astype(BF16)
        for lo in range(0, rows, BLOCK):
            t = lax.dot_general(w_qvg_t[...], a[lo:lo + BLOCK], NT, preferred_element_type=F32)
            for h in range(proj // head_dim):
                hs = slice(h * head_dim, (h + 1) * head_dim)
                q_scr[j, h, hs, lo:lo + BLOCK] = (t[hs] * (1.0 / math.sqrt(head_dim))).astype(BF16)
                v_scr[j, h, :, lo:lo + BLOCK] = t[proj:2 * proj][hs].astype(BF16)
                g_scr[j, h, :, lo:lo + BLOCK] = jax.nn.sigmoid(t[2 * proj:][hs])
        return 0

    lax.fori_loop(0, GROUP, one, 0)


def score_chunk(j, h, lo, kc, bias_scr, k_scr, q_scr):
    q_pad = q_scr[j, h, :, pl.ds(lo, BLOCK)]
    return jnp.dot(k_scr[j, kc:kc + KC], q_pad, preferred_element_type=F32) + bias_scr[h, kc:kc + KC, pl.ds(lo, BLOCK)]


def fold8(x, op):
    return op(x.reshape(x.shape[0] // 8, 8, x.shape[1]), axis=0)


def scores(j, h, lo, rows, bias_scr, k_scr, q_scr, s_scr, top_scr):
    top = None
    for kc in range(0, rows, KC):
        s = score_chunk(j, h, lo, kc, bias_scr, k_scr, q_scr)
        s_scr[h, kc:kc + KC] = s
        part = fold8(s, jnp.max)
        top = part if top is None else jnp.maximum(top, part)
    top_scr[h] = jnp.max(top, axis=0, keepdims=True)


def soft_and_next(j, lo, nj, nlo, h, rows, bias_scr, k_scr, q_scr, v_scr, g_scr, s_scr, top_scr, o_scr):
    top = top_scr[h]
    total = acc = ntop = None
    for kc in range(0, rows, KC):
        p = jnp.exp(s_scr[h, kc:kc + KC] - top)
        part = fold8(p, jnp.sum)
        total = part if total is None else total + part
        o = jnp.dot(v_scr[j, h, :, kc:kc + KC], p.astype(BF16), preferred_element_type=F32)
        acc = o if acc is None else acc + o
        s = score_chunk(nj, h, nlo, kc, bias_scr, k_scr, q_scr)
        s_scr[h, kc:kc + KC] = s
        part = fold8(s, jnp.max)
        ntop = part if ntop is None else jnp.maximum(ntop, part)
    top_scr[h] = jnp.max(ntop, axis=0, keepdims=True)
    total = jnp.sum(total, axis=0, keepdims=True)
    o_scr[j, h, :, pl.ds(lo, BLOCK)] = (g_scr[j, h, :, pl.ds(lo, BLOCK)] * (acc / total)).astype(BF16)


def swap_half(x):
    return pltpu.roll(x, HALF, 1)


def lower_half(shape):
    return lax.broadcasted_iota(jnp.int32, shape, len(shape) - 1) < HALF


def kernel(n_row, n_col, heads, z_ref, fill_ref, gamma_ref, beta_ref, w_k, w_qvg_t, w_b_t, w_o, out_ref,
           zown, zin, brecv, b_scr, a_scr, k_scr, q_scr, v_scr, g_scr, bias_scr, s_scr, top_scr, o_scr,
           own_sem, zin_sem, zsend_sem, bx_sem, bxs_sem, by_sem, bys_sem, bd_sem, bds_sem, out_sem, osend_sem):
    block, cols, chan = z_ref.shape
    rows = block * n_row
    share = cols // n_row
    n_group = share // GROUP
    head_dim = w_k.shape[1] // heads
    n_chip = n_row // 2
    me = lax.axis_index('row')
    my_col = lax.axis_index('col')
    mate = me + 1 - 2 * lax.rem(me, 2)
    gamma, beta = gamma_ref[...], beta_ref[...]

    def row_at(s):
        return lax.rem(me + s, n_row)

    def col_at(s):
        return lax.rem(my_col + s, n_col)

    own = [pltpu.make_async_copy(z_ref.at[pl.ds(q * (block // 4), block // 4)], zown.at[pl.ds(q * (block // 4), block // 4)], own_sem.at[q]) for q in range(4)]
    for cp in own:
        cp.start()

    barrier = pltpu.get_barrier_semaphore()
    for s in range(1, n_row):
        pl.semaphore_signal(barrier, inc=1, device_id={'row': row_at(s)}, device_id_type=MESH)
    for s in range(1, n_col):
        pl.semaphore_signal(barrier, inc=1, device_id={'col': col_at(s)}, device_id_type=MESH)
    pl.semaphore_wait(barrier, n_row + n_col - 2)

    my_rows = pl.ds(pl.multiple_of(me * block, block), block)

    def send_group(c):
        for s in range(1, n_row):
            to = row_at(s)
            pltpu.make_async_remote_copy(
                src_ref=z_ref.at[:, pl.ds(pl.multiple_of(to * share + c * GROUP, GROUP), GROUP), :],
                dst_ref=zin.at[c, my_rows], send_sem=zsend_sem.at[s], recv_sem=zin_sem.at[c],
                device_id={'row': to}, device_id_type=MESH).start()
        pltpu.make_async_copy(z_ref.at[:, pl.ds(pl.multiple_of(me * share + c * GROUP, GROUP), GROUP), :],
                              zin.at[c, my_rows], zin_sem.at[c]).start()

    send_group(0)

    per = 4

    def own_bias(t, _):
        for u in range(per):
            k = t * per + u
            a = layer_norm(zown[k].astype(F32), gamma, beta).astype(BF16)
            for half, lo in enumerate((0, cols - LANES)):
                b_scr[pl.ds(half * 8 * block + k, 8, stride=block), :] = lax.dot_general(
                    w_b_t[...], a[lo:lo + LANES], NT, preferred_element_type=F32)
        return 0

    for q in range(4):
        own[q].wait()
        lax.fori_loop(q * (block // 4 // per), (q + 1) * (block // 4 // per), own_bias, 0)

    low = lower_half((block, LANES))
    def own_part(half, h):
        return b_scr[half * 8 * block + h * block:half * 8 * block + (h + 1) * block, :]

    for h in range(heads):
        brecv[my_col, me, h] = own_part(0, h).astype(BF16)
    for h in range(0, heads, 2):
        brecv[my_col, me, heads + h // 2] = jnp.where(low, swap_half(own_part(1, h)), own_part(1, h + 1)).astype(BF16)

    def tile(c, r):
        return brecv.at[c, r]

    def to_chip(d):
        to = row_at(2 * d)
        return pltpu.make_async_remote_copy(src_ref=tile(my_col, me), dst_ref=tile(my_col, me), send_sem=bxs_sem.at[d],
                                            recv_sem=bx_sem.at[d], device_id={'row': to}, device_id_type=MESH)

    def to_col(e, d):
        r = row_at(n_row - 2 * d)
        return pltpu.make_async_remote_copy(src_ref=tile(my_col, r), dst_ref=tile(my_col, r), send_sem=bys_sem.at[e, d],
                                            recv_sem=by_sem.at[e, d], device_id={'col': col_at(e)}, device_id_type=MESH)

    def to_mate(e, d):
        c, r = col_at(n_col - e), row_at(n_row - 2 * d)
        return pltpu.make_async_remote_copy(src_ref=tile(c, r), dst_ref=tile(c, r), send_sem=bds_sem.at[e, d],
                                            recv_sem=bd_sem.at[e, d], device_id={'row': mate}, device_id_type=MESH)

    def forward(d):
        for e in range(1, n_col):
            to_col(e, d).start()
        to_mate(0, d).start()

    for d in range(1, n_chip):
        to_chip(d).start()
    forward(0)
    for c in range(1, n_group):
        send_group(c)

    q_scr[...] = jnp.zeros_like(q_scr)

    def prepare(c):
        pltpu.make_async_copy(zin.at[c], zin.at[c], zin_sem.at[c]).wait()
        norm_group(zin, c, gamma, beta, a_scr)
        project_group(rows, a_scr, w_k, w_qvg_t, k_scr, q_scr, v_scr, g_scr, head_dim)

    prepare(0)
    for d in range(1, n_chip):
        to_chip(d).wait_recv()
        forward(d)
    for d in range(n_chip):
        for e in range(1, n_col):
            to_col(e, d).wait_recv()
            to_mate(e, d).start()
    for e in range(n_col):
        for d in range(n_chip):
            to_mate(e, d).wait_recv()

    def widen(r, _):
        at = pl.ds(pl.multiple_of(r * block, block), block)
        fill = jnp.broadcast_to(fill_ref[at, :], (block, LANES))
        for c in range(0, n_col, 2):
            for h in range(heads):
                a0, a1 = brecv[c, r, h].astype(F32), swap_half(brecv[c + 1, r, h].astype(F32))
                b0, b1 = brecv[c, r, heads + h // 2].astype(F32), brecv[c + 1, r, heads + h // 2].astype(F32)
                if h % 2:
                    b0 = swap_half(b0)
                else:
                    b1 = swap_half(b1)
                lo = c * cols
                bias_scr[h, at, lo:lo + LANES] = a0 + fill
                bias_scr[h, at, lo + LANES:lo + 2 * LANES] = jnp.where(low, b0, a1) + fill
                bias_scr[h, at, lo + 2 * LANES:lo + 3 * LANES] = jnp.where(low, a1, b1) + fill
        return 0

    lax.fori_loop(0, n_row, widen, 0)

    n_block = rows // BLOCK
    first = me // 2

    def where(u):
        return lax.rem(u, GROUP), pl.multiple_of(lax.rem(u // GROUP + first, n_block) * BLOCK, BLOCK)

    def group(c, _):
        for h in range(heads):
            j, lo = where(0)
            scores(j, h, lo, rows, bias_scr, k_scr, q_scr, s_scr, top_scr)

        def one_block(b, _):
            def one(u, _):
                j, lo = where(u)
                nj, nlo = where(jnp.minimum(u + 1, GROUP * n_block - 1))
                for h in range(heads):
                    soft_and_next(j, lo, nj, nlo, h, rows, bias_scr, k_scr, q_scr, v_scr, g_scr, s_scr, top_scr, o_scr)
                return 0

            lax.fori_loop(b * GROUP, (b + 1) * GROUP, one, 0)
            _, lo = where(b * GROUP)

            def update(j, _):
                gated = o_scr[j, :, :, pl.ds(lo, BLOCK)].reshape(heads * head_dim, BLOCK)
                a_scr[pl.ds(lo * GROUP + j, BLOCK, stride=GROUP), :] = lax.dot_general(gated, w_o[...], TN, preferred_element_type=F32)
                return 0

            lax.fori_loop(0, GROUP, update, 0)

            def finish(t, _):
                at = pl.multiple_of(lo + t * HALF, HALF)
                upd = a_scr[pl.ds(pl.multiple_of(at * GROUP, HALF * GROUP), HALF * GROUP), :].reshape(HALF, GROUP, chan)
                zin[c, pl.ds(at, HALF)] = (zin[c, pl.ds(at, HALF)].astype(F32) + upd).astype(BF16)
                return 0

            lax.fori_loop(0, BLOCK // HALF, finish, 0)

            def send(t, _):
                seg = lo // PIECE + t
                to = seg // (block // PIECE)
                off = lax.rem(seg, block // PIECE) * PIECE
                src = zin.at[c, pl.ds(pl.multiple_of(seg * PIECE, PIECE), PIECE)]
                dst = out_ref.at[pl.ds(pl.multiple_of(off, PIECE), PIECE), pl.ds(pl.multiple_of(me * share + c * GROUP, GROUP), GROUP), :]

                @pl.when(to == me)
                def _():
                    pltpu.make_async_copy(src, dst, out_sem).start()

                @pl.when(to != me)
                def _():
                    pltpu.make_async_remote_copy(src_ref=src, dst_ref=dst, send_sem=osend_sem, recv_sem=out_sem,
                                                 device_id={'row': to}, device_id_type=MESH).start()
                return 0

            lax.fori_loop(0, BLOCK // PIECE, send, 0)
            return 0

        lax.fori_loop(0, n_block, one_block, 0)

        @pl.when(c < n_group - 1)
        def _():
            prepare(c + 1)
        return 0

    lax.fori_loop(0, n_group, group, 0)

    for s in range(1, n_row):
        pltpu.make_async_copy(z_ref.at[:, 0:share, :], z_ref.at[:, 0:share, :], zsend_sem.at[s]).wait()
    for d in range(1, n_chip):
        to_chip(d).wait_send()
    for d in range(n_chip):
        for e in range(1, n_col):
            to_col(e, d).wait_send()
        for e in range(n_col):
            to_mate(e, d).wait_send()
    pltpu.make_async_copy(zin.at[:, 0:rows - block], zin.at[:, 0:rows - block], osend_sem).wait()
    pltpu.make_async_copy(z_ref, out_ref, out_sem).wait()


def run(n_row, n_col, z, fill, gamma, beta, w_k, w_qvg_t, w_b_t, w_o, heads):
    block, cols, chan = z.shape
    rows, share, proj = block * n_row, cols // n_row, w_k.shape[1]
    n_group, n_chip, head_dim = share // GROUP, n_row // 2, proj // heads
    vmem = pl.BlockSpec(memory_space=pltpu.VMEM)
    hbm = pl.BlockSpec(memory_space=pl.ANY)
    dma = pltpu.SemaphoreType.DMA
    return pl.pallas_call(
        functools.partial(kernel, n_row, n_col, heads),
        out_shape=jax.ShapeDtypeStruct(z.shape, BF16),
        in_specs=[hbm] + [vmem] * 7,
        out_specs=hbm,
        scratch_shapes=[
            pltpu.VMEM((block, cols, chan), BF16),
            pltpu.VMEM((n_group, rows, GROUP, chan), BF16),
            pltpu.VMEM((n_col, n_row, heads + heads // 2, block, LANES), BF16),
            pltpu.VMEM((2 * 8 * block, LANES), F32),
            pltpu.VMEM((rows * GROUP, chan), F32),
            pltpu.VMEM((GROUP, rows, proj), BF16),
            pltpu.VMEM((GROUP, heads, proj, rows), BF16),
            pltpu.VMEM((GROUP, heads, head_dim, rows), BF16),
            pltpu.VMEM((GROUP, heads, head_dim, rows), F32),
            pltpu.VMEM((heads, rows, rows), F32),
            pltpu.VMEM((heads, rows, BLOCK), F32),
            pltpu.VMEM((heads, 1, BLOCK), F32),
            pltpu.VMEM((GROUP, heads, head_dim, rows), BF16),
            dma((4,)), dma((n_group,)), dma((n_row,)), dma((n_chip,)), dma((n_chip,)), dma((n_col, n_chip)), dma((n_col, n_chip)),
            dma((n_col, n_chip)), dma((n_col, n_chip)), dma, dma,
        ],
        compiler_params=pltpu.CompilerParams(vmem_limit_bytes=62 * 1024 * 1024, collective_id=0, has_side_effects=True),
        name="triangle",
    )(z, fill, gamma, beta, w_k, w_qvg_t, w_b_t, w_o)


def solution(mesh):
    n_row, n_col = mesh.shape['row'], mesh.shape['col']

    def body(pair_tile, res_mask, ln_gamma, ln_beta, w_q, w_k, w_v, w_b, w_g, w_o):
        heads = w_b.shape[1]
        fill = jnp.where(res_mask > 0, 0.0, MASK_FILL).astype(F32)[:, None]
        w_qvg_t = jnp.concatenate([w_q.T, w_v.T, w_g.T], axis=0)
        w_b_t = jnp.pad(w_b.T, ((0, 8 - heads), (0, 0)))
        return run(n_row, n_col, pair_tile, fill, ln_gamma[None], ln_beta[None], w_k, w_qvg_t, w_b_t, w_o, heads)

    tile_spec = P(('data', 'row'), 'col', None)
    return jax.shard_map(body, mesh=mesh, in_specs=(tile_spec, P('data'), P(), P(), P(), P(), P(), P(), P(), P()), out_specs=tile_spec, check_vma=False)
```

time: 307 us -> 170 us (0.55)
  waiting for transfers between devices: 78.4 us -> 0 us
  Pallas kernels: 98.9 us -> 159 us
  blocking collectives: 58.8 us -> 0 us
  local copies, waits for them, and re-layouts: 31.4 us -> 9.6 us
  between operations: 13.6 us -> 0.03 us
  other arithmetic: 11.4 us -> 1.34 us
  matrix products: 8.64 us -> 0 us
  starting transfers between devices: 5.08 us -> 0 us
    pallas_call x1, Pallas kernels: 98.9 us -> 159 us  [run(): pl.pallas_call(functools.partial(kernel, n_row, n_col, heads), out_shape=...]
    all_to_all x1 -> x0, blocking collectives: 58.8 us -> none  [body(): return lax.all_to_all(out_t, 'row', 0, 1, tiled=True)]
    all_to_all x1 -> x0, waiting for transfers between devices: 52.2 us -> none  [body(): z_t = lax.all_to_all(pair_tile, 'row', 1, 0, tiled=True)]
    all_gather x2 -> x0, waiting for transfers between devices: 26.1 us -> none  [the longest x1 26.1 us: body(): bias = lax.all_gather(bias, 'row', axis=1, tiled=True)]
    all_gather x2 -> x0, local copies, waits for them, and re-layouts: 12.6 us -> none  [the longest x1 8.46 us: body(): bias = lax.all_gather(bias, 'col', axis=2, tiled=True)]
    reduce_sum x2 -> x0, other arithmetic: 10.7 us -> none  [the longest x1 6.42 us: layer_norm(): variance = jnp.mean(centred * centred, axis=-1, keepdims=True)]
    all_to_all x2 -> x0, local copies, waits for them, and re-layouts: 9.88 us -> none  [the longest x1 6.35 us: body(): z_t = lax.all_to_all(pair_tile, 'row', 1, 0, tiled=True)]
    dot_general x1 -> x0, matrix products: 8.64 us -> none  [body(): jnp.einsum('kic,ch->hki', normed, w_b, preferred_element_type=F32)]
  transfers between devices with their start and end apart: 3 -> 0, of which waited for: 2 -> 0; matrix products, arithmetic and copies ran while one was open for 5% -> 0% of each run, Pallas kernels for 0% -> 0%
where the time goes in v3:
time: 170 us
  Pallas kernels  159 us (94%)
  local copies, waits for them, and re-layouts  9.6 us (6%)
    pallas_call x1, Pallas kernels, run(): pl.pallas_call(functools.partial(kernel, n_row, n_col, heads), out_shape=...  159 us
    unnamed x4, local copies, waits for them, and re-layouts  7.45 us

profile of v3, /device:TPU:97, one launch (start us, length us, event | category | flops | bytes accessed | tf_op | source)
XLA Modules:
  0.0 169.8 jit_solution(5540459383287996837)
XLA Ops:
  0.0 1.2 pad.4.w_b_t
  1.2 0.7 compare_select_fusion
  1.9 0.9 copy.14
  2.8 0.9 copy.15
  3.7 0.9 copy.16
  4.6 0.7 pad_maximum_fusion.w_qvg_t
  5.2 0.9 broadcast_in_dim.22.fill_ref
  6.1 158.9 %triangle.1 = bf16[96,192,128]{2,1,0:T(8,128)(2,1)} custom-call(bf16[96,192,128]{2,1,0:T(8,128)(2,1)} %z_ref.1, f32[768,1]{1,0:T(8,128)} %broadcast_in_dim.22.fill_ref, f32[1,128]{1,0:T(1,128)} %bitcast.10, f32[1,128]{1,0:T(1,128)} %bitcast.11, bf16[128,128]{1,0:T(8,128)(2,1)} %w_k.1, bf16[384,128]{1,0:T(8,128)(2,1)} %pad_maximum_fusion.w_qvg_t, ...), custom_call_target="tpu_custom_call" | custom-call | tf_op jit(solution)/shard_map/triangle/pallas_call | solution.py:329
  165.0 4.8 %copy.19 = bf16[96,192,128]{2,1,0:T(8,128)(2,1)} copy(bf16[96,192,128]{2,1,0:T(8,128)(2,1)} %triangle.1) | data formatting | bytes 9437184

commit v4 on v3

--- a/solution.py
+++ b/solution.py
@@ -104,8 +104,8 @@
     return lax.broadcasted_iota(jnp.int32, shape, len(shape) - 1) < HALF
 
 
-def kernel(n_row, n_col, heads, z_ref, fill_ref, gamma_ref, beta_ref, w_k, w_qvg_t, w_b_t, w_o, out_ref,
-           zown, zin, brecv, b_scr, a_scr, k_scr, q_scr, v_scr, g_scr, bias_scr, s_scr, top_scr, o_scr,
+def kernel(n_row, n_col, heads, z_ref, mask_ref, gamma_ref, beta_ref, w_q, w_k, w_v, w_b, w_g, w_o, out_ref,
+           w_qvg_t, w_b_t, fill_scr, zown, zin, brecv, b_scr, a_scr, k_scr, q_scr, v_scr, g_scr, bias_scr, s_scr, top_scr, o_scr,
            own_sem, zin_sem, zsend_sem, bx_sem, bxs_sem, by_sem, bys_sem, bd_sem, bds_sem, out_sem, osend_sem):
     block, cols, chan = z_ref.shape
     rows = block * n_row
@@ -128,6 +128,17 @@
     for cp in own:
         cp.start()
 
+    proj = heads * head_dim
+    for n, w in enumerate((w_q, w_v, w_g)):
+        w_qvg_t[n * proj:(n + 1) * proj] = w[...].astype(F32).T.astype(BF16)
+    eye = (lax.broadcasted_iota(jnp.int32, (chan, chan), 0) == lax.broadcasted_iota(jnp.int32, (chan, chan), 1)).astype(BF16)
+    w_b_t[...] = jnp.zeros_like(w_b_t)
+    w_b_t[0:heads] = lax.dot_general(w_b[...], eye, TN, preferred_element_type=F32).astype(BF16)
+    fill_row = jnp.where(mask_ref[...] > 0, 0.0, MASK_FILL).astype(F32)
+    for lo in range(0, rows, LANES):
+        fill_scr[lo:lo + LANES] = jnp.broadcast_to(fill_row[:, lo:lo + LANES], (LANES, LANES)).T
+    q_scr[...] = jnp.zeros_like(q_scr)
+
     barrier = pltpu.get_barrier_semaphore()
     for s in range(1, n_row):
         pl.semaphore_signal(barrier, inc=1, device_id={'row': row_at(s)}, device_id_type=MESH)
@@ -135,21 +146,19 @@
         pl.semaphore_signal(barrier, inc=1, device_id={'col': col_at(s)}, device_id_type=MESH)
     pl.semaphore_wait(barrier, n_row + n_col - 2)
 
-    my_rows = pl.ds(pl.multiple_of(me * block, block), block)
-
-    def send_group(c):
+    def send_group(c, lo=0, n=block):
         for s in range(1, n_row):
             to = row_at(s)
             pltpu.make_async_remote_copy(
-                src_ref=z_ref.at[:, pl.ds(pl.multiple_of(to * share + c * GROUP, GROUP), GROUP), :],
-                dst_ref=zin.at[c, my_rows], send_sem=zsend_sem.at[s], recv_sem=zin_sem.at[c],
+                src_ref=z_ref.at[lo:lo + n, pl.ds(pl.multiple_of(to * share + c * GROUP, GROUP), GROUP), :],
+                dst_ref=zin.at[c, pl.ds(pl.multiple_of(me * block + lo, 16), n)], send_sem=zsend_sem.at[s], recv_sem=zin_sem.at[c],
                 device_id={'row': to}, device_id_type=MESH).start()
-        pltpu.make_async_copy(z_ref.at[:, pl.ds(pl.multiple_of(me * share + c * GROUP, GROUP), GROUP), :],
-                              zin.at[c, my_rows], zin_sem.at[c]).start()
-
-    send_group(0)
-
-    per = 4
+        pltpu.make_async_copy(z_ref.at[lo:lo + n, pl.ds(pl.multiple_of(me * share + c * GROUP, GROUP), GROUP), :],
+                              zin.at[c, pl.ds(pl.multiple_of(me * block + lo, 16), n)], zin_sem.at[c]).start()
+
+    send_group(0, 0, block // 2)
+
+    per = 8
 
     def own_bias(t, _):
         for u in range(per):
@@ -181,78 +190,118 @@
         return pltpu.make_async_remote_copy(src_ref=tile(my_col, me), dst_ref=tile(my_col, me), send_sem=bxs_sem.at[d],
                                             recv_sem=bx_sem.at[d], device_id={'row': to}, device_id_type=MESH)
 
+    def line(d):
+        return row_at(n_row - 2 * d)
+
     def to_col(e, d):
-        r = row_at(n_row - 2 * d)
-        return pltpu.make_async_remote_copy(src_ref=tile(my_col, r), dst_ref=tile(my_col, r), send_sem=bys_sem.at[e, d],
-                                            recv_sem=by_sem.at[e, d], device_id={'col': col_at(e)}, device_id_type=MESH)
+        t = tile(my_col, line(d))
+        return pltpu.make_async_remote_copy(src_ref=t, dst_ref=t, send_sem=bys_sem.at[e, d], recv_sem=by_sem.at[e, d],
+                                            device_id={'col': col_at(e)}, device_id_type=MESH)
+
+    def relay(d):
+        e = 1 if d < n_chip // 2 else n_col - 1
+        t = tile(col_at(n_col - e), line(d))
+        return pltpu.make_async_remote_copy(src_ref=t, dst_ref=t, send_sem=bys_sem.at[2, d], recv_sem=by_sem.at[2, d],
+                                            device_id={'col': col_at(e)}, device_id_type=MESH)
 
     def to_mate(e, d):
-        c, r = col_at(n_col - e), row_at(n_row - 2 * d)
-        return pltpu.make_async_remote_copy(src_ref=tile(c, r), dst_ref=tile(c, r), send_sem=bds_sem.at[e, d],
-                                            recv_sem=bd_sem.at[e, d], device_id={'row': mate}, device_id_type=MESH)
+        t = tile(col_at(n_col - e), line(d))
+        return pltpu.make_async_remote_copy(src_ref=t, dst_ref=t, send_sem=bds_sem.at[e, d], recv_sem=bd_sem.at[e, d],
+                                            device_id={'row': mate}, device_id_type=MESH)
+
+    near = (1, n_col - 1)
 
     def forward(d):
-        for e in range(1, n_col):
+        for e in near:
             to_col(e, d).start()
         to_mate(0, d).start()
 
     for d in range(1, n_chip):
         to_chip(d).start()
     forward(0)
+    send_group(0, block // 2, block // 2)
     for c in range(1, n_group):
         send_group(c)
 
-    q_scr[...] = jnp.zeros_like(q_scr)
+    def widen(col):
+        def rows_of(r, _, c):
+            at = pl.ds(pl.multiple_of(r * block, block), block)
+            fill = fill_scr[at]
+            lo = c * cols
+            for h in range(heads):
+                a, b = brecv[c, r, h].astype(F32), brecv[c, r, heads + h // 2].astype(F32)
+                if c % 2 == 0:
+                    bias_scr[h, at, lo:lo + LANES] = a + fill
+                    b = (swap_half(b) if h % 2 else b) + fill
+                    bias_scr[h, at, lo + LANES:lo + LANES + HALF] = b[:, 0:HALF]
+                else:
+                    a = swap_half(a)
+                    b = b if h % 2 else swap_half(b)
+                    bias_scr[h, at, lo:lo + HALF] = (a + fill)[:, HALF:LANES]
+                    bias_scr[h, at, lo + HALF:lo + HALF + LANES] = jnp.where(low, a, b) + fill
+            return 0
+
+        for c in range(n_col):
+            @pl.when(col == c)
+            def _():
+                lax.fori_loop(0, n_row, functools.partial(rows_of, c=c), 0)
 
     def prepare(c):
         pltpu.make_async_copy(zin.at[c], zin.at[c], zin_sem.at[c]).wait()
         norm_group(zin, c, gamma, beta, a_scr)
         project_group(rows, a_scr, w_k, w_qvg_t, k_scr, q_scr, v_scr, g_scr, head_dim)
 
-    prepare(0)
     for d in range(1, n_chip):
         to_chip(d).wait_recv()
         forward(d)
     for d in range(n_chip):
-        for e in range(1, n_col):
+        for e in near:
             to_col(e, d).wait_recv()
             to_mate(e, d).start()
-    for e in range(n_col):
+        relay(d).start()
+    prepare(0)
+    for e in (0,) + near:
         for d in range(n_chip):
             to_mate(e, d).wait_recv()
 
-    def widen(r, _):
-        at = pl.ds(pl.multiple_of(r * block, block), block)
-        fill = jnp.broadcast_to(fill_ref[at, :], (block, LANES))
-        for c in range(0, n_col, 2):
-            for h in range(heads):
-                a0, a1 = brecv[c, r, h].astype(F32), swap_half(brecv[c + 1, r, h].astype(F32))
-                b0, b1 = brecv[c, r, heads + h // 2].astype(F32), brecv[c + 1, r, heads + h // 2].astype(F32)
-                if h % 2:
-                    b0 = swap_half(b0)
-                else:
-                    b1 = swap_half(b1)
-                lo = c * cols
-                bias_scr[h, at, lo:lo + LANES] = a0 + fill
-                bias_scr[h, at, lo + LANES:lo + 2 * LANES] = jnp.where(low, b0, a1) + fill
-                bias_scr[h, at, lo + 2 * LANES:lo + 3 * LANES] = jnp.where(low, a1, b1) + fill
+    def widen_near(t, _):
+        widen(lax.rem(my_col + t + t // 2, n_col))
         return 0
 
-    lax.fori_loop(0, n_row, widen, 0)
+    lax.fori_loop(0, 3, widen_near, 0)
+
+    def far_to_mate():
+        for d in range(n_chip):
+            relay(d).wait_recv()
+            to_mate(2, d).start()
+
+    def far_ready():
+        for d in range(n_chip):
+            to_mate(2, d).wait_recv()
+        widen(col_at(2))
 
     n_block = rows // BLOCK
-    first = me // 2
-
-    def where(u):
-        return lax.rem(u, GROUP), pl.multiple_of(lax.rem(u // GROUP + first, n_block) * BLOCK, BLOCK)
 
     def group(c, _):
+        first = jnp.where(c == 0, (my_col + 1) // 2, me // 2)
+
+        def where(u):
+            return lax.rem(u, GROUP), pl.multiple_of(lax.rem(u // GROUP + first, n_block) * BLOCK, BLOCK)
+
         for h in range(heads):
             j, lo = where(0)
             scores(j, h, lo, rows, bias_scr, k_scr, q_scr, s_scr, top_scr)
 
         def one_block(b, _):
             def one(u, _):
+                @pl.when((c == 0) & (u == GROUP // 2 - 1))
+                def _():
+                    far_to_mate()
+
+                @pl.when((c == 0) & (u == GROUP - 2))
+                def _():
+                    far_ready()
+
                 j, lo = where(u)
                 nj, nlo = where(jnp.minimum(u + 1, GROUP * n_block - 1))
                 for h in range(heads):
@@ -311,17 +360,19 @@
     for d in range(1, n_chip):
         to_chip(d).wait_send()
     for d in range(n_chip):
-        for e in range(1, n_col):
+        for e in near:
             to_col(e, d).wait_send()
+        relay(d).wait_send()
         for e in range(n_col):
             to_mate(e, d).wait_send()
     pltpu.make_async_copy(zin.at[:, 0:rows - block], zin.at[:, 0:rows - block], osend_sem).wait()
     pltpu.make_async_copy(z_ref, out_ref, out_sem).wait()
 
 
-def run(n_row, n_col, z, fill, gamma, beta, w_k, w_qvg_t, w_b_t, w_o, heads):
+def run(n_row, n_col, z, mask, gamma, beta, w_q, w_k, w_v, w_b, w_g, w_o):
     block, cols, chan = z.shape
     rows, share, proj = block * n_row, cols // n_row, w_k.shape[1]
+    heads = w_b.shape[1]
     n_group, n_chip, head_dim = share // GROUP, n_row // 2, proj // heads
     vmem = pl.BlockSpec(memory_space=pltpu.VMEM)
     hbm = pl.BlockSpec(memory_space=pl.ANY)
@@ -329,9 +380,12 @@
     return pl.pallas_call(
         functools.partial(kernel, n_row, n_col, heads),
         out_shape=jax.ShapeDtypeStruct(z.shape, BF16),
-        in_specs=[hbm] + [vmem] * 7,
+        in_specs=[hbm] + [vmem] * 9,
         out_specs=hbm,
         scratch_shapes=[
+            pltpu.VMEM((3 * proj, chan), BF16),
+            pltpu.VMEM((8, chan), BF16),
+            pltpu.VMEM((rows, LANES), F32),
             pltpu.VMEM((block, cols, chan), BF16),
             pltpu.VMEM((n_group, rows, GROUP, chan), BF16),
             pltpu.VMEM((n_col, n_row, heads + heads // 2, block, LANES), BF16),
@@ -350,18 +404,14 @@
         ],
         compiler_params=pltpu.CompilerParams(vmem_limit_bytes=62 * 1024 * 1024, collective_id=0, has_side_effects=True),
         name="triangle",
-    )(z, fill, gamma, beta, w_k, w_qvg_t, w_b_t, w_o)
+    )(z, mask, gamma, beta, w_q, w_k, w_v, w_b, w_g, w_o)
 
 
 def solution(mesh):
     n_row, n_col = mesh.shape['row'], mesh.shape['col']
 
     def body(pair_tile, res_mask, ln_gamma, ln_beta, w_q, w_k, w_v, w_b, w_g, w_o):
-        heads = w_b.shape[1]
-        fill = jnp.where(res_mask > 0, 0.0, MASK_FILL).astype(F32)[:, None]
-        w_qvg_t = jnp.concatenate([w_q.T, w_v.T, w_g.T], axis=0)
-        w_b_t = jnp.pad(w_b.T, ((0, 8 - heads), (0, 0)))
-        return run(n_row, n_col, pair_tile, fill, ln_gamma[None], ln_beta[None], w_k, w_qvg_t, w_b_t, w_o, heads)
+        return run(n_row, n_col, pair_tile, res_mask[None], ln_gamma[None], ln_beta[None], w_q, w_k, w_v, w_b, w_g, w_o)
 
     tile_spec = P(('data', 'row'), 'col', None)
     return jax.shard_map(body, mesh=mesh, in_specs=(tile_spec, P('data'), P(), P(), P(), P(), P(), P(), P(), P()), out_specs=tile_spec, check_vma=False)

time: 170 us -> 160 us (0.941)
  Pallas kernels: 159 us -> 151 us
  local copies, waits for them, and re-layouts: 9.6 us -> 7.51 us
    pallas_call x1, Pallas kernels: 159 us -> 151 us  [run(): pl.pallas_call(functools.partial(kernel, n_row, n_col, heads), out_shape=...]
    unnamed x4 -> x2, local copies, waits for them, and re-layouts: 7.45 us -> 6.25 us
where the time goes in v4:
time: 160 us; the launch traced here: 159 us
  Pallas kernels  151 us (94%)
  local copies, waits for them, and re-layouts  7.51 us (5%)
    pallas_call x1, Pallas kernels, run(): pl.pallas_call(functools.partial(kernel, n_row, n_col, heads), out_shape=...  151 us
    unnamed x2, local copies, waits for them, and re-layouts  6.25 us

profile of v4, /device:TPU:97, one launch (start us, length us, event | category | flops | bytes accessed | tf_op | source)
XLA Modules:
  0.0 158.9 jit_solution(18346783511205551709)
XLA Ops:
  0.0 1.3 broadcast_in_dim.9.mask_ref
  1.3 1.4 copy.11.w_b
  2.7 151.4 %triangle.1 = bf16[96,192,128]{2,1,0:T(8,128)(2,1)} custom-call(bf16[96,192,128]{2,1,0:T(8,128)(2,1)} %z_ref.1, s32[1,768]{1,0:T(1,128)} %broadcast_in_dim.9.mask_ref, f32[1,128]{1,0:T(1,128)} %bitcast.2, f32[1,128]{1,0:T(1,128)} %bitcast.3, bf16[128,128]{1,0:T(8,128)(2,1)} %w_q.1, bf16[128,128]{1,0:T(8,128)(2,1)} %w_k.1, bf16[128,128]{1,0:T(8,128)(2,1)} %w_v.1, ...), custom_call_target="tpu_custom_call" | custom-call | tf_op jit(solution)/shard_map/triangle/pallas_call | solution.py:380
  154.0 4.8 %copy.13 = bf16[96,192,128]{2,1,0:T(8,128)(2,1)} copy(bf16[96,192,128]{2,1,0:T(8,128)(2,1)} %triangle.1) | data formatting | bytes 9437184

commit v5 on v4

--- a/solution.py
+++ b/solution.py
@@ -8,13 +8,15 @@
 from jax.sharding import PartitionSpec as P
 
 LN_EPS = 1e-5
-MASK_FILL = -1e9
+FILL_PARTS = (-998244352.0, -1753088.0, -2560.0)
+assert sum(FILL_PARTS) == -1e9
 GROUP = 8
 BLOCK = 256
 PIECE = 32
-KC = 256
+KC = 384
 LANES = 128
 HALF = 64
+UNROLL = 2
 F32 = jnp.float32
 BF16 = jnp.bfloat16
 NT = (((1,), (1,)), ((), ()))
@@ -41,59 +43,84 @@
     lax.fori_loop(0, rows // step, one, 0)
 
 
-def project_group(rows, a_scr, w_k, w_qvg_t, k_scr, q_scr, v_scr, g_scr, head_dim):
-    proj = w_k.shape[1]
-
-    def one(j, _):
-        a = a_scr[pl.ds(j, rows, stride=GROUP), :].astype(BF16)
-        k_scr[j] = jnp.dot(a, w_k[...], preferred_element_type=F32).astype(BF16)
-        for lo in range(0, rows, BLOCK):
-            t = lax.dot_general(w_qvg_t[...], a[lo:lo + BLOCK], NT, preferred_element_type=F32)
-            for h in range(proj // head_dim):
-                hs = slice(h * head_dim, (h + 1) * head_dim)
-                q_scr[j, h, hs, lo:lo + BLOCK] = (t[hs] * (1.0 / math.sqrt(head_dim))).astype(BF16)
-                v_scr[j, h, :, lo:lo + BLOCK] = t[proj:2 * proj][hs].astype(BF16)
-                g_scr[j, h, :, lo:lo + BLOCK] = jax.nn.sigmoid(t[2 * proj:][hs])
+def project_group(rows, a_scr, w_kk, w_qvg_t, fill_scr, k_scr, q_scr, v_scr, g_scr, head_dim):
+    proj = w_qvg_t.shape[0] // 3
+    heads = proj // head_dim
+
+    def one(pair, _):
+        cols = []
+        for side in range(2):
+            j = 2 * pair + side
+            a = a_scr[pl.ds(j, rows, stride=GROUP), :].astype(BF16)
+            cols.append(a)
+            for lo in range(0, rows, 2 * LANES):
+                t = lax.dot_general(w_qvg_t[...], a[lo:lo + 2 * LANES], NT, preferred_element_type=F32)
+                for h in range(heads):
+                    hs = slice(h * head_dim, (h + 1) * head_dim)
+                    q = (t[hs] * (1.0 / math.sqrt(head_dim))).astype(BF16)
+                    here = slice(side * head_dim, (side + 1) * head_dim)
+                    for n in range(2):
+                        q_scr[pair, h, lo // LANES + n, here, side * LANES:(side + 1) * LANES] = q[:, n * LANES:(n + 1) * LANES]
+                    v_scr[pair, h, here, lo:lo + 2 * LANES] = t[proj:2 * proj][hs].astype(BF16)
+                    g_scr[j, h, :, lo:lo + 2 * LANES] = jax.nn.sigmoid(t[2 * proj:][hs])
+        a = jnp.concatenate(cols, axis=1)
+        for lo in range(0, rows, 2 * LANES):
+            fill = fill_scr[lo:lo + 2 * LANES]
+            for h in range(0, heads, 2):
+                k = jnp.dot(a[lo:lo + 2 * LANES], w_kk[:, h * LANES:(h + 2) * LANES], preferred_element_type=F32).astype(BF16)
+                k_scr[pair, h, lo:lo + 2 * LANES] = k[:, 0:LANES] + fill
+                k_scr[pair, h + 1, lo:lo + 2 * LANES] = k[:, LANES:2 * LANES] + fill
         return 0
 
-    lax.fori_loop(0, GROUP, one, 0)
-
-
-def score_chunk(j, h, lo, kc, bias_scr, k_scr, q_scr):
-    q_pad = q_scr[j, h, :, pl.ds(lo, BLOCK)]
-    return jnp.dot(k_scr[j, kc:kc + KC], q_pad, preferred_element_type=F32) + bias_scr[h, kc:kc + KC, pl.ds(lo, BLOCK)]
+    lax.fori_loop(0, GROUP // 2, one, 0)
+
+
+def right_side(pair, h, ib, q_scr, tail_scr):
+    return jnp.concatenate([q_scr[pair, h, ib], tail_scr[...]], axis=0)
+
+
+def score_chunk(pair, h, ib, kc, right, bias_scr, k_scr):
+    left = jnp.concatenate([k_scr[pair, h, kc:kc + KC], bias_scr[h, ib, kc:kc + KC]], axis=1)
+    return jnp.dot(left, right, preferred_element_type=F32)
 
 
 def fold8(x, op):
     return op(x.reshape(x.shape[0] // 8, 8, x.shape[1]), axis=0)
 
 
-def scores(j, h, lo, rows, bias_scr, k_scr, q_scr, s_scr, top_scr):
+def scores(pair, ib, h, rows, tail_scr, bias_scr, k_scr, q_scr, s_scr, top_scr):
     top = None
+    right = right_side(pair, h, ib, q_scr, tail_scr)
     for kc in range(0, rows, KC):
-        s = score_chunk(j, h, lo, kc, bias_scr, k_scr, q_scr)
+        s = score_chunk(pair, h, ib, kc, right, bias_scr, k_scr)
         s_scr[h, kc:kc + KC] = s
         part = fold8(s, jnp.max)
         top = part if top is None else jnp.maximum(top, part)
     top_scr[h] = jnp.max(top, axis=0, keepdims=True)
 
 
-def soft_and_next(j, lo, nj, nlo, h, rows, bias_scr, k_scr, q_scr, v_scr, g_scr, s_scr, top_scr, o_scr):
+def soft_and_next(pair, ib, npair, nib, h, rows, tail_scr, bias_scr, k_scr, q_scr, v_scr, g_scr, s_scr, top_scr, o_scr):
+    head_dim = g_scr.shape[2]
     top = top_scr[h]
     total = acc = ntop = None
+    right = right_side(npair, h, nib, q_scr, tail_scr)
     for kc in range(0, rows, KC):
         p = jnp.exp(s_scr[h, kc:kc + KC] - top)
         part = fold8(p, jnp.sum)
         total = part if total is None else total + part
-        o = jnp.dot(v_scr[j, h, :, kc:kc + KC], p.astype(BF16), preferred_element_type=F32)
+        o = jnp.dot(v_scr[pair, h, :, kc:kc + KC], p.astype(BF16), preferred_element_type=F32)
         acc = o if acc is None else acc + o
-        s = score_chunk(nj, h, nlo, kc, bias_scr, k_scr, q_scr)
+        s = score_chunk(npair, h, nib, kc, right, bias_scr, k_scr)
         s_scr[h, kc:kc + KC] = s
         part = fold8(s, jnp.max)
         ntop = part if ntop is None else jnp.maximum(ntop, part)
     top_scr[h] = jnp.max(ntop, axis=0, keepdims=True)
     total = jnp.sum(total, axis=0, keepdims=True)
-    o_scr[j, h, :, pl.ds(lo, BLOCK)] = (g_scr[j, h, :, pl.ds(lo, BLOCK)] * (acc / total)).astype(BF16)
+    at = pl.ds(pl.multiple_of(ib * LANES, LANES), LANES)
+    for side in range(2):
+        lanes = slice(side * LANES, (side + 1) * LANES)
+        o = acc[side * head_dim:(side + 1) * head_dim, lanes] / total[:, lanes]
+        o_scr[2 * pair + side, h, :, at] = (g_scr[2 * pair + side, h, :, at] * o).astype(BF16)
 
 
 def swap_half(x):
@@ -105,7 +132,7 @@
 
 
 def kernel(n_row, n_col, heads, z_ref, mask_ref, gamma_ref, beta_ref, w_q, w_k, w_v, w_b, w_g, w_o, out_ref,
-           w_qvg_t, w_b_t, fill_scr, zown, zin, brecv, b_scr, a_scr, k_scr, q_scr, v_scr, g_scr, bias_scr, s_scr, top_scr, o_scr,
+           w_qvg_t, w_b_t, w_kk, tail_scr, fill_scr, zown, zin, brecv, b_scr, a_scr, k_scr, q_scr, v_scr, g_scr, bias_scr, s_scr, top_scr, o_scr,
            own_sem, zin_sem, zsend_sem, bx_sem, bxs_sem, by_sem, bys_sem, bd_sem, bds_sem, out_sem, osend_sem):
     block, cols, chan = z_ref.shape
     rows = block * n_row
@@ -134,9 +161,22 @@
     eye = (lax.broadcasted_iota(jnp.int32, (chan, chan), 0) == lax.broadcasted_iota(jnp.int32, (chan, chan), 1)).astype(BF16)
     w_b_t[...] = jnp.zeros_like(w_b_t)
     w_b_t[0:heads] = lax.dot_general(w_b[...], eye, TN, preferred_element_type=F32).astype(BF16)
-    fill_row = jnp.where(mask_ref[...] > 0, 0.0, MASK_FILL).astype(F32)
+    w_kk[...] = jnp.zeros_like(w_kk)
+    for h in range(heads):
+        wide = w_k[:, h * head_dim:(h + 1) * head_dim]
+        w_kk[0:chan, h * LANES:h * LANES + head_dim] = wide
+        w_kk[chan:2 * chan, h * LANES + head_dim:h * LANES + 2 * head_dim] = wide
+    row = lax.broadcasted_iota(jnp.int32, (LANES - 2 * head_dim, 2 * LANES), 0)
+    tail_scr[0:LANES - 2 * head_dim] = jnp.where(row < len(FILL_PARTS), 1.0, 0.0).astype(BF16)
+    tail_scr[LANES - 2 * head_dim:] = jnp.concatenate([eye, eye], axis=1)
+    lane = lax.broadcasted_iota(jnp.int32, (LANES, LANES), 1)
+    part = jnp.zeros((LANES, LANES), F32)
+    for n, f in enumerate(FILL_PARTS):
+        part = jnp.where(lane == 2 * head_dim + n, f, part)
+    keep = mask_ref[...].astype(F32)
     for lo in range(0, rows, LANES):
-        fill_scr[lo:lo + LANES] = jnp.broadcast_to(fill_row[:, lo:lo + LANES], (LANES, LANES)).T
+        masked = jnp.broadcast_to(keep[:, lo:lo + LANES], (LANES, LANES)).T
+        fill_scr[lo:lo + LANES] = jnp.where(masked > 0.5, 0.0, part).astype(BF16)
     q_scr[...] = jnp.zeros_like(q_scr)
 
     barrier = pltpu.get_barrier_semaphore()
@@ -226,19 +266,20 @@
     def widen(col):
         def rows_of(r, _, c):
             at = pl.ds(pl.multiple_of(r * block, block), block)
-            fill = fill_scr[at]
-            lo = c * cols
+            first = c * cols // LANES
             for h in range(heads):
-                a, b = brecv[c, r, h].astype(F32), brecv[c, r, heads + h // 2].astype(F32)
                 if c % 2 == 0:
-                    bias_scr[h, at, lo:lo + LANES] = a + fill
-                    b = (swap_half(b) if h % 2 else b) + fill
-                    bias_scr[h, at, lo + LANES:lo + LANES + HALF] = b[:, 0:HALF]
+                    bias_scr[h, first, at] = brecv[c, r, h]
+                    b = brecv[c, r, heads + h // 2]
+                    if h % 2:
+                        b = swap_half(b.astype(F32)).astype(BF16)
+                    bias_scr[h, first + 1, at, 0:HALF] = b[:, 0:HALF]
                 else:
-                    a = swap_half(a)
+                    a = swap_half(brecv[c, r, h].astype(F32))
+                    b = brecv[c, r, heads + h // 2].astype(F32)
                     b = b if h % 2 else swap_half(b)
-                    bias_scr[h, at, lo:lo + HALF] = (a + fill)[:, HALF:LANES]
-                    bias_scr[h, at, lo + HALF:lo + HALF + LANES] = jnp.where(low, a, b) + fill
+                    bias_scr[h, first, at, HALF:LANES] = a.astype(BF16)[:, HALF:LANES]
+                    bias_scr[h, first + 1, at] = jnp.where(low, a, b).astype(BF16)
             return 0
 
         for c in range(n_col):
@@ -249,7 +290,7 @@
     def prepare(c):
         pltpu.make_async_copy(zin.at[c], zin.at[c], zin_sem.at[c]).wait()
         norm_group(zin, c, gamma, beta, a_scr)
-        project_group(rows, a_scr, w_k, w_qvg_t, k_scr, q_scr, v_scr, g_scr, head_dim)
+        project_group(rows, a_scr, w_kk, w_qvg_t, fill_scr, k_scr, q_scr, v_scr, g_scr, head_dim)
 
     for d in range(1, n_chip):
         to_chip(d).wait_recv()
@@ -285,31 +326,36 @@
     def group(c, _):
         first = jnp.where(c == 0, (my_col + 1) // 2, me // 2)
 
+        def block_lo(b):
+            return pl.multiple_of(lax.rem(b + first, n_block) * BLOCK, BLOCK)
+
         def where(u):
-            return lax.rem(u, GROUP), pl.multiple_of(lax.rem(u // GROUP + first, n_block) * BLOCK, BLOCK)
+            v = lax.rem(u, GROUP)
+            return lax.rem(v, GROUP // 2), block_lo(u // GROUP) // LANES + v // (GROUP // 2)
 
         for h in range(heads):
-            j, lo = where(0)
-            scores(j, h, lo, rows, bias_scr, k_scr, q_scr, s_scr, top_scr)
+            pair, ib = where(0)
+            scores(pair, ib, h, rows, tail_scr, bias_scr, k_scr, q_scr, s_scr, top_scr)
 
         def one_block(b, _):
             def one(u, _):
-                @pl.when((c == 0) & (u == GROUP // 2 - 1))
+                @pl.when((c == 0) & (u == (GROUP // 2 - 2) // UNROLL))
                 def _():
                     far_to_mate()
 
-                @pl.when((c == 0) & (u == GROUP - 2))
+                @pl.when((c == 0) & (u == (GROUP - 2) // UNROLL))
                 def _():
                     far_ready()
 
-                j, lo = where(u)
-                nj, nlo = where(jnp.minimum(u + 1, GROUP * n_block - 1))
-                for h in range(heads):
-                    soft_and_next(j, lo, nj, nlo, h, rows, bias_scr, k_scr, q_scr, v_scr, g_scr, s_scr, top_scr, o_scr)
+                for v in range(UNROLL):
+                    pair, ib = where(u * UNROLL + v)
+                    npair, nib = where(jnp.minimum(u * UNROLL + v + 1, GROUP * n_block - 1))
+                    for h in range(heads):
+                        soft_and_next(pair, ib, npair, nib, h, rows, tail_scr, bias_scr, k_scr, q_scr, v_scr, g_scr, s_scr, top_scr, o_scr)
                 return 0
 
-            lax.fori_loop(b * GROUP, (b + 1) * GROUP, one, 0)
-            _, lo = where(b * GROUP)
+            lax.fori_loop(b * (GROUP // UNROLL), (b + 1) * (GROUP // UNROLL), one, 0)
+            lo = block_lo(b)
 
             def update(j, _):
                 gated = o_scr[j, :, :, pl.ds(lo, BLOCK)].reshape(heads * head_dim, BLOCK)
@@ -385,17 +431,19 @@
         scratch_shapes=[
             pltpu.VMEM((3 * proj, chan), BF16),
             pltpu.VMEM((8, chan), BF16),
-            pltpu.VMEM((rows, LANES), F32),
+            pltpu.VMEM((2 * chan, heads * LANES), BF16),
+            pltpu.VMEM((2 * LANES - 2 * head_dim, 2 * LANES), BF16),
+            pltpu.VMEM((rows, LANES), BF16),
             pltpu.VMEM((block, cols, chan), BF16),
             pltpu.VMEM((n_group, rows, GROUP, chan), BF16),
             pltpu.VMEM((n_col, n_row, heads + heads // 2, block, LANES), BF16),
             pltpu.VMEM((2 * 8 * block, LANES), F32),
             pltpu.VMEM((rows * GROUP, chan), F32),
-            pltpu.VMEM((GROUP, rows, proj), BF16),
-            pltpu.VMEM((GROUP, heads, proj, rows), BF16),
-            pltpu.VMEM((GROUP, heads, head_dim, rows), BF16),
+            pltpu.VMEM((GROUP // 2, heads, rows, LANES), BF16),
+            pltpu.VMEM((GROUP // 2, heads, rows // LANES, 2 * head_dim, 2 * LANES), BF16),
+            pltpu.VMEM((GROUP // 2, heads, 2 * head_dim, rows), BF16),
             pltpu.VMEM((GROUP, heads, head_dim, rows), F32),
-            pltpu.VMEM((heads, rows, rows), F32),
+            pltpu.VMEM((heads, rows // LANES, rows, LANES), BF16),
             pltpu.VMEM((heads, rows, BLOCK), F32),
             pltpu.VMEM((heads, 1, BLOCK), F32),
             pltpu.VMEM((GROUP, heads, head_dim, rows), BF16),

time: 160 us -> 154 us (0.963)
  Pallas kernels: 151 us -> 146 us
    pallas_call x1, Pallas kernels: 151 us -> 146 us  [run(): pl.pallas_call(functools.partial(kernel, n_row, n_col, heads), out_shape=...]
where the time goes in v5:
time: 154 us
  Pallas kernels  146 us (95%)
  local copies, waits for them, and re-layouts  7.51 us (5%)
    pallas_call x1, Pallas kernels, run(): pl.pallas_call(functools.partial(kernel, n_row, n_col, heads), out_shape=...  146 us
    unnamed x2, local copies, waits for them, and re-layouts  6.25 us

profile of v5, /device:TPU:97, one launch (start us, length us, event | category | flops | bytes accessed | tf_op | source)
XLA Modules:
  0.0 153.7 jit_solution(15919856782744739129)
XLA Ops:
  0.0 1.3 broadcast_in_dim.9.mask_ref
  1.3 1.4 copy.11.w_b
  2.7 146.2 %triangle.1 = bf16[96,192,128]{2,1,0:T(8,128)(2,1)} custom-call(bf16[96,192,128]{2,1,0:T(8,128)(2,1)} %z_ref.1, s32[1,768]{1,0:T(1,128)} %broadcast_in_dim.9.mask_ref, f32[1,128]{1,0:T(1,128)} %bitcast.2, f32[1,128]{1,0:T(1,128)} %bitcast.3, bf16[128,128]{1,0:T(8,128)(2,1)} %w_q.1, bf16[128,128]{1,0:T(8,128)(2,1)} %w_k.1, bf16[128,128]{1,0:T(8,128)(2,1)} %w_v.1, ...), custom_call_target="tpu_custom_call" | custom-call | tf_op jit(solution)/shard_map/triangle/pallas_call | solution.py:426
  148.9 4.8 %copy.13 = bf16[96,192,128]{2,1,0:T(8,128)(2,1)} copy(bf16[96,192,128]{2,1,0:T(8,128)(2,1)} %triangle.1) | data formatting | bytes 9437184

commit v6 on v5

--- a/solution.py
+++ b/solution.py
@@ -160,7 +160,7 @@
         w_qvg_t[n * proj:(n + 1) * proj] = w[...].astype(F32).T.astype(BF16)
     eye = (lax.broadcasted_iota(jnp.int32, (chan, chan), 0) == lax.broadcasted_iota(jnp.int32, (chan, chan), 1)).astype(BF16)
     w_b_t[...] = jnp.zeros_like(w_b_t)
-    w_b_t[0:heads] = lax.dot_general(w_b[...], eye, TN, preferred_element_type=F32).astype(BF16)
+    w_b_t[0:heads] = w_b[...]
     w_kk[...] = jnp.zeros_like(w_kk)
     for h in range(heads):
         wide = w_k[:, h * head_dim:(h + 1) * head_dim]
@@ -174,9 +174,9 @@
     for n, f in enumerate(FILL_PARTS):
         part = jnp.where(lane == 2 * head_dim + n, f, part)
     keep = mask_ref[...].astype(F32)
-    for lo in range(0, rows, LANES):
-        masked = jnp.broadcast_to(keep[:, lo:lo + LANES], (LANES, LANES)).T
-        fill_scr[lo:lo + LANES] = jnp.where(masked > 0.5, 0.0, part).astype(BF16)
+    for n in range(rows // LANES):
+        masked = jnp.broadcast_to(keep[n:n + 1], (LANES, LANES)).T
+        fill_scr[n * LANES:(n + 1) * LANES] = jnp.where(masked > 0.5, 0.0, part).astype(BF16)
     q_scr[...] = jnp.zeros_like(q_scr)
 
     barrier = pltpu.get_barrier_semaphore()
@@ -259,9 +259,6 @@
     for d in range(1, n_chip):
         to_chip(d).start()
     forward(0)
-    send_group(0, block // 2, block // 2)
-    for c in range(1, n_group):
-        send_group(c)
 
     def widen(col):
         def rows_of(r, _, c):
@@ -287,19 +284,24 @@
             def _():
                 lax.fori_loop(0, n_row, functools.partial(rows_of, c=c), 0)
 
+    def arrived(c):
+        pltpu.make_async_copy(zin.at[c], zin.at[c], zin_sem.at[c]).wait()
+
     def prepare(c):
-        pltpu.make_async_copy(zin.at[c], zin.at[c], zin_sem.at[c]).wait()
         norm_group(zin, c, gamma, beta, a_scr)
         project_group(rows, a_scr, w_kk, w_qvg_t, fill_scr, k_scr, q_scr, v_scr, g_scr, head_dim)
 
     for d in range(1, n_chip):
         to_chip(d).wait_recv()
         forward(d)
+    send_group(0, block // 2, block // 2)
     for d in range(n_chip):
         for e in near:
             to_col(e, d).wait_recv()
             to_mate(e, d).start()
         relay(d).start()
+    arrived(0)
+    send_group(1)
     prepare(0)
     for e in (0,) + near:
         for d in range(n_chip):
@@ -346,6 +348,11 @@
                 @pl.when((c == 0) & (u == (GROUP - 2) // UNROLL))
                 def _():
                     far_ready()
+
+                @pl.when((c == 0) & (u == (GROUP + GROUP // 2) // UNROLL))
+                def _():
+                    for g in range(2, n_group):
+                        send_group(g)
 
                 for v in range(UNROLL):
                     pair, ib = where(u * UNROLL + v)
@@ -396,6 +403,7 @@
 
         @pl.when(c < n_group - 1)
         def _():
+            arrived(c + 1)
             prepare(c + 1)
         return 0
 
@@ -418,7 +426,7 @@
 def run(n_row, n_col, z, mask, gamma, beta, w_q, w_k, w_v, w_b, w_g, w_o):
     block, cols, chan = z.shape
     rows, share, proj = block * n_row, cols // n_row, w_k.shape[1]
-    heads = w_b.shape[1]
+    heads = w_b.shape[0]
     n_group, n_chip, head_dim = share // GROUP, n_row // 2, proj // heads
     vmem = pl.BlockSpec(memory_space=pltpu.VMEM)
     hbm = pl.BlockSpec(memory_space=pl.ANY)
@@ -459,7 +467,7 @@
     n_row, n_col = mesh.shape['row'], mesh.shape['col']
 
     def body(pair_tile, res_mask, ln_gamma, ln_beta, w_q, w_k, w_v, w_b, w_g, w_o):
-        return run(n_row, n_col, pair_tile, res_mask[None], ln_gamma[None], ln_beta[None], w_q, w_k, w_v, w_b, w_g, w_o)
+        return run(n_row, n_col, pair_tile, res_mask.reshape(-1, LANES), ln_gamma[None], ln_beta[None], w_q, w_k, w_v, w_b.T, w_g, w_o)
 
     tile_spec = P(('data', 'row'), 'col', None)
     return jax.shard_map(body, mesh=mesh, in_specs=(tile_spec, P('data'), P(), P(), P(), P(), P(), P(), P(), P()), out_specs=tile_spec, check_vma=False)

time: 154 us -> 151 us (0.981)
  local copies, waits for them, and re-layouts: 7.51 us -> 4.84 us
    unnamed x2 -> x1, local copies, waits for them, and re-layouts: 6.25 us -> 4.84 us
where the time goes in v6:
time: 151 us
  Pallas kernels  146 us (97%)
  local copies, waits for them, and re-layouts  4.84 us (3%)
    pallas_call x1, Pallas kernels, run(): pl.pallas_call(functools.partial(kernel, n_row, n_col, heads), out_shape=...  146 us
    unnamed x1, local copies, waits for them, and re-layouts  4.84 us

profile of v6, /device:TPU:97, one launch (start us, length us, event | category | flops | bytes accessed | tf_op | source)
XLA Modules:
  0.0 151.0 jit_solution(17151541791340189775)
XLA Ops:
  0.0 146.1 %triangle.1 = bf16[96,192,128]{2,1,0:T(8,128)(2,1)} custom-call(bf16[96,192,128]{2,1,0:T(8,128)(2,1)} %z_ref.1, s32[6,128]{1,0:T(8,128)} %bitcast.4, f32[1,128]{1,0:T(1,128)} %bitcast.6, f32[1,128]{1,0:T(1,128)} %bitcast.7, bf16[128,128]{1,0:T(8,128)(2,1)} %w_q.1, bf16[128,128]{1,0:T(8,128)(2,1)} %w_k.1, bf16[128,128]{1,0:T(8,128)(2,1)} %w_v.1, ...), custom_call_target="tpu_custom_call" | custom-call | tf_op jit(solution)/shard_map/triangle/pallas_call | solution.py:434
  146.1 4.8 %copy.12 = bf16[96,192,128]{2,1,0:T(8,128)(2,1)} copy(bf16[96,192,128]{2,1,0:T(8,128)(2,1)} %triangle.1) | data formatting | bytes 9437184

commit v7 on v6

--- a/solution.py
+++ b/solution.py
@@ -196,7 +196,8 @@
         pltpu.make_async_copy(z_ref.at[lo:lo + n, pl.ds(pl.multiple_of(me * share + c * GROUP, GROUP), GROUP), :],
                               zin.at[c, pl.ds(pl.multiple_of(me * block + lo, 16), n)], zin_sem.at[c]).start()
 
-    send_group(0, 0, block // 2)
+    early = block * 2 // 3
+    send_group(0, 0, early)
 
     per = 8
 
@@ -291,10 +292,10 @@
         norm_group(zin, c, gamma, beta, a_scr)
         project_group(rows, a_scr, w_kk, w_qvg_t, fill_scr, k_scr, q_scr, v_scr, g_scr, head_dim)
 
-    for d in range(1, n_chip):
+    for d in sorted(range(1, n_chip), key=lambda d: min(d, n_chip - d)):
         to_chip(d).wait_recv()
         forward(d)
-    send_group(0, block // 2, block // 2)
+    send_group(0, early, block - early)
     for d in range(n_chip):
         for e in near:
             to_col(e, d).wait_recv()
@@ -323,17 +324,18 @@
             to_mate(2, d).wait_recv()
         widen(col_at(2))
 
-    n_block = rows // BLOCK
+    n_block = rows // LANES
+    n_pair = GROUP // 2
+    per_block = n_pair // UNROLL
 
     def group(c, _):
         first = jnp.where(c == 0, (my_col + 1) // 2, me // 2)
 
-        def block_lo(b):
-            return pl.multiple_of(lax.rem(b + first, n_block) * BLOCK, BLOCK)
+        def block_at(b):
+            return lax.rem(b // 2 + first, n_block // 2) * 2 + lax.rem(b, 2)
 
         def where(u):
-            v = lax.rem(u, GROUP)
-            return lax.rem(v, GROUP // 2), block_lo(u // GROUP) // LANES + v // (GROUP // 2)
+            return lax.rem(u, n_pair), block_at(u // n_pair)
 
         for h in range(heads):
             pair, ib = where(0)
@@ -349,27 +351,19 @@
                 def _():
                     far_ready()
 
-                @pl.when((c == 0) & (u == (GROUP + GROUP // 2) // UNROLL))
-                def _():
-                    for g in range(2, n_group):
-                        send_group(g)
-
                 for v in range(UNROLL):
                     pair, ib = where(u * UNROLL + v)
-                    npair, nib = where(jnp.minimum(u * UNROLL + v + 1, GROUP * n_block - 1))
+                    npair, nib = where(jnp.minimum(u * UNROLL + v + 1, n_pair * n_block - 1))
                     for h in range(heads):
                         soft_and_next(pair, ib, npair, nib, h, rows, tail_scr, bias_scr, k_scr, q_scr, v_scr, g_scr, s_scr, top_scr, o_scr)
                 return 0
 
-            lax.fori_loop(b * (GROUP // UNROLL), (b + 1) * (GROUP // UNROLL), one, 0)
-            lo = block_lo(b)
-
-            def update(j, _):
-                gated = o_scr[j, :, :, pl.ds(lo, BLOCK)].reshape(heads * head_dim, BLOCK)
-                a_scr[pl.ds(lo * GROUP + j, BLOCK, stride=GROUP), :] = lax.dot_general(gated, w_o[...], TN, preferred_element_type=F32)
-                return 0
-
-            lax.fori_loop(0, GROUP, update, 0)
+            lax.fori_loop(b * per_block, (b + 1) * per_block, one, 0)
+            lo = pl.multiple_of(block_at(b) * LANES, LANES)
+
+            for j in range(GROUP):
+                gated = o_scr[j, :, :, pl.ds(lo, LANES)].reshape(heads * head_dim, LANES)
+                a_scr[pl.ds(lo * GROUP + j, LANES, stride=GROUP), :] = lax.dot_general(gated, w_o[...], TN, preferred_element_type=F32)
 
             def finish(t, _):
                 at = pl.multiple_of(lo + t * HALF, HALF)
@@ -377,7 +371,7 @@
                 zin[c, pl.ds(at, HALF)] = (zin[c, pl.ds(at, HALF)].astype(F32) + upd).astype(BF16)
                 return 0
 
-            lax.fori_loop(0, BLOCK // HALF, finish, 0)
+            lax.fori_loop(0, LANES // HALF, finish, 0)
 
             def send(t, _):
                 seg = lo // PIECE + t
@@ -396,7 +390,7 @@
                                                  device_id={'row': to}, device_id_type=MESH).start()
                 return 0
 
-            lax.fori_loop(0, BLOCK // PIECE, send, 0)
+            lax.fori_loop(0, LANES // PIECE, send, 0)
             return 0
 
         lax.fori_loop(0, n_block, one_block, 0)
@@ -404,6 +398,11 @@
         @pl.when(c < n_group - 1)
         def _():
             arrived(c + 1)
+
+            @pl.when(c < n_group - 2)
+            def _():
+                send_group(c + 2)
+
             prepare(c + 1)
         return 0
 

time: 151 us -> 146 us (0.967)
  the two profiles are of different devices: /device:TPU:97 before, /device:TPU:101 now
where the time goes in v7:
time: 146 us; the launch traced here: 145 us
  Pallas kernels  140 us (96%)
  local copies, waits for them, and re-layouts  4.84 us (3%)
    pallas_call x1, Pallas kernels, run(): pl.pallas_call(functools.partial(kernel, n_row, n_col, heads), out_shape=...  140 us
    unnamed x1, local copies, waits for them, and re-layouts  4.84 us

profile of v7, /device:TPU:101, one launch (start us, length us, event | category | flops | bytes accessed | tf_op | source)
XLA Modules:
  0.0 145.3 jit_solution(17350727398519915792)
XLA Ops:
  0.0 140.5 %triangle.1 = bf16[96,192,128]{2,1,0:T(8,128)(2,1)} custom-call(bf16[96,192,128]{2,1,0:T(8,128)(2,1)} %z_ref.1, s32[6,128]{1,0:T(8,128)} %bitcast.4, f32[1,128]{1,0:T(1,128)} %bitcast.6, f32[1,128]{1,0:T(1,128)} %bitcast.7, bf16[128,128]{1,0:T(8,128)(2,1)} %w_q.1, bf16[128,128]{1,0:T(8,128)(2,1)} %w_k.1, bf16[128,128]{1,0:T(8,128)(2,1)} %w_v.1, ...), custom_call_target="tpu_custom_call" | custom-call | tf_op jit(solution)/shard_map/triangle/pallas_call | solution.py:433
  140.5 4.8 %copy.12 = bf16[96,192,128]{2,1,0:T(8,128)(2,1)} copy(bf16[96,192,128]{2,1,0:T(8,128)(2,1)} %triangle.1) | data formatting | bytes 9437184

commit v8 on v7

--- a/solution.py
+++ b/solution.py
@@ -297,22 +297,26 @@
         forward(d)
     send_group(0, early, block - early)
     for d in range(n_chip):
+        to_mate(0, d).wait_recv()
+    widen(my_col)
+    arrived(0)
+    send_group(1)
+    norm_group(zin, 0, gamma, beta, a_scr)
+    for d in range(n_chip):
         for e in near:
             to_col(e, d).wait_recv()
             to_mate(e, d).start()
         relay(d).start()
-    arrived(0)
-    send_group(1)
-    prepare(0)
-    for e in (0,) + near:
+    project_group(rows, a_scr, w_kk, w_qvg_t, fill_scr, k_scr, q_scr, v_scr, g_scr, head_dim)
+    for e in near:
         for d in range(n_chip):
             to_mate(e, d).wait_recv()
 
     def widen_near(t, _):
-        widen(lax.rem(my_col + t + t // 2, n_col))
+        widen(lax.rem(my_col + 1 + t * (n_col - 2), n_col))
         return 0
 
-    lax.fori_loop(0, 3, widen_near, 0)
+    lax.fori_loop(0, 2, widen_near, 0)
 
     def far_to_mate():
         for d in range(n_chip):
@@ -462,11 +466,41 @@
     )(z, mask, gamma, beta, w_q, w_k, w_v, w_b, w_g, w_o)
 
 
+def copy_out(x, pieces=8):
+    step = x.shape[0] // pieces
+
+    def body(x_ref, o_ref, buf, in_sem, out_sem):
+        def part(n):
+            return pl.ds(n * step, step)
+
+        loads = [pltpu.make_async_copy(x_ref.at[part(n)], buf.at[part(n)], in_sem.at[n]) for n in range(pieces)]
+        stores = [pltpu.make_async_copy(buf.at[part(n)], o_ref.at[part(n)], out_sem.at[n]) for n in range(pieces)]
+        for load in loads:
+            load.start()
+        for load, store in zip(loads, stores):
+            load.wait()
+            store.start()
+        for store in stores:
+            store.wait()
+
+    hbm = pl.BlockSpec(memory_space=pltpu.HBM)
+    return pl.pallas_call(
+        body,
+        out_shape=jax.ShapeDtypeStruct(x.shape, x.dtype),
+        in_specs=[hbm],
+        out_specs=hbm,
+        scratch_shapes=[pltpu.VMEM(x.shape, x.dtype), pltpu.SemaphoreType.DMA((pieces,)), pltpu.SemaphoreType.DMA((pieces,))],
+        compiler_params=pltpu.CompilerParams(vmem_limit_bytes=62 * 1024 * 1024),
+        name="copy_out",
+    )(x)
+
+
 def solution(mesh):
     n_row, n_col = mesh.shape['row'], mesh.shape['col']
 
     def body(pair_tile, res_mask, ln_gamma, ln_beta, w_q, w_k, w_v, w_b, w_g, w_o):
-        return run(n_row, n_col, pair_tile, res_mask.reshape(-1, LANES), ln_gamma[None], ln_beta[None], w_q, w_k, w_v, w_b.T, w_g, w_o)
+        out = run(n_row, n_col, pair_tile, res_mask.reshape(-1, LANES), ln_gamma[None], ln_beta[None], w_q, w_k, w_v, w_b.T, w_g, w_o)
+        return copy_out(out)
 
     tile_spec = P(('data', 'row'), 'col', None)
     return jax.shard_map(body, mesh=mesh, in_specs=(tile_spec, P('data'), P(), P(), P(), P(), P(), P(), P(), P()), out_specs=tile_spec, check_vma=False)

time: 146 us -> 144 us (0.986)
  local copies, waits for them, and re-layouts: 4.84 us -> 0 us
  Pallas kernels: 140 us -> 144 us
    unnamed x1 -> x0, local copies, waits for them, and re-layouts: 4.84 us -> none
    pallas_call x0 -> x1, Pallas kernels: none -> 4.12 us  [copy_out(): pl.pallas_call(body, out_shape=jax.ShapeDtypeStruct(x.shape, x.dtype), in...]
where the time goes in v8:
time: 144 us
  Pallas kernels  144 us (100%)
    pallas_call x1, Pallas kernels, run(): pl.pallas_call(functools.partial(kernel, n_row, n_col, heads), out_shape=...  140 us
    pallas_call x1, Pallas kernels, copy_out(): pl.pallas_call(body, out_shape=jax.ShapeDtypeStruct(x.shape, x.dtype), in...  4.12 us

profile of v8, /device:TPU:101, one launch (start us, length us, event | category | flops | bytes accessed | tf_op | source)
XLA Modules:
  0.0 143.9 jit_solution(7949786089641288049)
XLA Ops:
  0.0 139.8 %triangle.1.x_ref = bf16[96,192,128]{2,1,0:T(8,128)(2,1)} custom-call(bf16[96,192,128]{2,1,0:T(8,128)(2,1)} %z_ref.1, s32[6,128]{1,0:T(8,128)} %bitcast.4, f32[1,128]{1,0:T(1,128)} %bitcast.6, f32[1,128]{1,0:T(1,128)} %bitcast.7, bf16[128,128]{1,0:T(8,128)(2,1)} %w_q.1, bf16[128,128]{1,0:T(8,128)(2,1)} %w_k.1, bf16[128,128]{1,0:T(8,128)(2,1)} %w_v.1, ...), custom_call_target="tpu_custom_call" | custom-call | tf_op jit(solution)/shard_map/triangle/pallas_call | solution.py:437
  139.8 4.1 %copy_out.1 = bf16[96,192,128]{2,1,0:T(8,128)(2,1)} custom-call(bf16[96,192,128]{2,1,0:T(8,128)(2,1)} %triangle.1.x_ref), custom_call_target="tpu_custom_call" | custom-call | tf_op jit(solution)/shard_map/copy_out/pallas_call | solution.py:487

commit v9 on v8

--- a/solution.py
+++ b/solution.py
@@ -333,10 +333,13 @@
     per_block = n_pair // UNROLL
 
     def group(c, _):
-        first = jnp.where(c == 0, (my_col + 1) // 2, me // 2)
+        first = (my_col + 1) // 2
+        chip = me // 2
+        last = chip + (chip + 1) // 2
 
         def block_at(b):
-            return lax.rem(b // 2 + first, n_block // 2) * 2 + lax.rem(b, 2)
+            paired = lax.rem(b // 2 + first, n_block // 2) * 2 + lax.rem(b, 2)
+            return jnp.where(c == 0, paired, lax.rem(b + last + 1, n_block))
 
         def where(u):
             return lax.rem(u, n_pair), block_at(u // n_pair)

time: 144 us -> 144 us (level)
  no operation moved by 1% of the time
where the time goes in v9:
time: 144 us
  Pallas kernels  144 us (100%)
    pallas_call x1, Pallas kernels, run(): pl.pallas_call(functools.partial(kernel, n_row, n_col, heads), out_shape=...  140 us
    pallas_call x1, Pallas kernels, copy_out(): pl.pallas_call(body, out_shape=jax.ShapeDtypeStruct(x.shape, x.dtype), in...  4.12 us

profile of v9, /device:TPU:101, one launch (start us, length us, event | category | flops | bytes accessed | tf_op | source)
XLA Modules:
  0.0 144.1 jit_solution(297255115465756765)
XLA Ops:
  0.0 140.0 %triangle.1.x_ref = bf16[96,192,128]{2,1,0:T(8,128)(2,1)} custom-call(bf16[96,192,128]{2,1,0:T(8,128)(2,1)} %z_ref.1, s32[6,128]{1,0:T(8,128)} %bitcast.4, f32[1,128]{1,0:T(1,128)} %bitcast.6, f32[1,128]{1,0:T(1,128)} %bitcast.7, bf16[128,128]{1,0:T(8,128)(2,1)} %w_q.1, bf16[128,128]{1,0:T(8,128)(2,1)} %w_k.1, bf16[128,128]{1,0:T(8,128)(2,1)} %w_v.1, ...), custom_call_target="tpu_custom_call" | custom-call | tf_op jit(solution)/shard_map/triangle/pallas_call | solution.py:440
  140.0 4.1 %copy_out.1 = bf16[96,192,128]{2,1,0:T(8,128)(2,1)} custom-call(bf16[96,192,128]{2,1,0:T(8,128)(2,1)} %triangle.1.x_ref), custom_call_target="tpu_custom_call" | custom-call | tf_op jit(solution)/shard_map/copy_out/pallas_call | solution.py:490
